TPU v7x, 16 devices: a whole 2x2x2 slice. The times are simulated.
16 devices in a mesh: model: 2 (over z), data: 8 (over y, x, core).
Axes of the slice: x: 2, y: 2, z: 2, core: 2. Of those that a mesh axis runs over, the one named last changes fastest.
Arguments:
- tokens: bfloat16 [16384, 768], P('data')
- w_up: bfloat16 [768, 3072], P(None, 'model')
- w_down: bfloat16 [3072, 768], P('model')
- task_heads: bfloat16 [4, 768, 3], replicated
- labels: int32 [4, 16384], P(None, 'data')
Outputs:
- output 1: float32 [4], replicated
- output 2: float32 [768, 3072], P('data', 'model')
- output 3: float32 [3072, 768], P(('model', 'data'))
All inputs are finite; a program needn't handle non-finite values.
Results may differ from a plain program's by a relative error of at most 0.001.
Values are sent between devices in bfloat16 or wider.
A program may use at most 1 GiB of HBM per device.

v0:
```python
import jax
import jax.numpy as jnp
from jax import lax
from jax.sharding import PartitionSpec as P

STEPS = 20


def simplex_weights(gram_mat):
    n_task = gram_mat.shape[0]
    trace_scale = jnp.trace(gram_mat) / n_task

    def eg_step(step_idx, weights):
        updated = weights * jnp.exp(-jnp.sum(gram_mat * weights[None, :], axis=1) / trace_scale)
        return updated / jnp.sum(updated)

    return lax.fori_loop(0, STEPS, eg_step, jnp.full((n_task,), 1.0 / n_task, jnp.float32))


def solution(mesh):
    n_data = mesh.shape['data']

    def local_step(tokens, w_up, w_down, task_heads, labels):
        n_total = tokens.shape[0] * n_data
        n_class = task_heads.shape[2]
        pre_act = jnp.dot(tokens, w_up, preferred_element_type=jnp.float32)
        act_val, gelu_slope = jax.jvp(jax.nn.gelu, (pre_act,), (jnp.ones_like(pre_act),))
        act_bf = act_val.astype(jnp.bfloat16)
        part_out = jnp.dot(act_bf, w_down, preferred_element_type=jnp.float32)
        mlp_out = lax.psum(part_out, 'model')
        trunk_out = (tokens.astype(jnp.float32) + mlp_out).astype(jnp.bfloat16)
        logits = jnp.einsum('bd,tdc->tbc', trunk_out, task_heads, preferred_element_type=jnp.float32)
        class_prob = jax.nn.softmax(logits, axis=-1)
        onehot = jax.nn.one_hot(labels, n_class, dtype=jnp.float32)
        dlogit = (class_prob - onehot) / n_total
        d_trunk = jnp.einsum('tbc,tdc->tbd', dlogit, task_heads.astype(jnp.float32), precision=lax.Precision.HIGHEST).astype(jnp.bfloat16)
        g_down = jnp.einsum('bf,tbd->tfd', act_bf, d_trunk, preferred_element_type=jnp.float32)
        d_act = jnp.einsum('tbd,fd->tbf', d_trunk, w_down, preferred_element_type=jnp.float32)
        d_pre = (d_act * gelu_slope[None]).astype(jnp.bfloat16)
        g_up = jnp.einsum('bd,tbf->tdf', tokens, d_pre, preferred_element_type=jnp.float32)
        up_shard = lax.psum_scatter(g_up, 'data', scatter_dimension=1, tiled=True)
        down_shard = lax.psum_scatter(g_down, 'data', scatter_dimension=1, tiled=True)
        gram_part = (jnp.einsum('tij,sij->ts', up_shard, up_shard, precision=lax.Precision.HIGHEST)
                     + jnp.einsum('tij,sij->ts', down_shard, down_shard, precision=lax.Precision.HIGHEST))
        gram_mat = lax.psum(gram_part, ('model', 'data'))
        task_weights = simplex_weights(gram_mat)
        grad_up = jnp.einsum('t,tij->ij', task_weights, up_shard, precision=lax.Precision.HIGHEST)
        grad_down = jnp.einsum('t,tij->ij', task_weights, down_shard, precision=lax.Precision.HIGHEST)
        return task_weights, grad_up, grad_down

    return jax.shard_map(
        local_step, mesh=mesh,
        in_specs=(P('data', None), P(None, 'model'), P('model', None), P(None, None, None), P(None, 'data')),
        out_specs=(P(None), P('data', 'model'), P(('model', 'data'), None)),
        check_vma=False)
```

profile of v0, /device:TPU:1, one launch (start us, length us, event | category | flops | bytes accessed | tf_op | source)
XLA Modules:
  0.0 877.6 jit_solution(3627045535300170290)
XLA Ops:
  7.2 15.0 %fusion.9 = (f32[2048,1536]{1,0:T(8,128)}, f32[2048,1536]{1,0:T(8,128)S(1)}) fusion(bf16[2048,768]{1,0:T(8,128)(2,1)} %param.7, bf16[768,1536]{1,0:T(8,128)(2,1)} %param.8), kind=kOutput, calls=%fused_computation.16 | convolution fusion | flops 4882169856 | bytes 30670848 | tf_op jit(solution)/shard_map/dot_general | solution.py:26
  22.2 4.6 copy-done.8
  26.8 9.1 %fusion.48 = f32[2048,768]{1,0:T(8,128)} fusion(bf16[1536,768]{1,0:T(8,128)(2,1)S(1)} %copy-done, f32[2048,1536]{1,0:T(8,128)S(1)} %get-tuple-element.56), kind=kOutput, calls=%fused_computation.56 | convolution fusion | flops 4860149760 | bytes 21233664 | tf_op jit(solution)/shard_map/dot_general | solution.py:29
  36.4 12.6 %copy.18 = f32[2048,1536]{0,1:T(8,128)} copy(f32[2048,1536]{1,0:T(8,128)} %get-tuple-element.55) | data formatting | bytes 25165824 | tf_op jit(solution)/shard_map/jvp()/add_any | solution.py:27
  49.0 137.9 %all-reduce.6.cloned.1.call-done = f32[2048,768]{1,0:T(8,128)} async-done(((f32[2048,768]{1,0:T(8,128)}), f32[2048,768]{1,0:T(8,128)}) %all-reduce.6.cloned.1.call-update) | async-done | bytes 6291472 | tf_op jit(solution)/shard_map/psum | solution.py:30
  186.9 4.7 fusion.50
  191.7 10.8 %convolution_convert_fusion = bf16[4,2048,768]{2,1,0:T(8,128)(2,1)S(1)} fusion(f32[4,2048,3]{1,0,2:T(4,128)S(1)} %fusion.39, bf16[4,768,3]{1,0,2:T(4,128)(2,1)S(1)} %copy-done.4), kind=kOutput, calls=%fused_computation.20 | convolution fusion | flops 232783872 | bytes 12699648 | tf_op jit(solution)/shard_map/tbc,tdc->tbd/dot_general | solution.py:36
  202.5 4.5 copy-done.2
  207.0 26.3 %convolution_bitcast_fusion = f32[4,1536,768]{1,2,0:T(8,128)} fusion(bf16[4,2048,768]{2,1,0:T(8,128)(2,1)S(1)} %convolution_convert_fusion, f32[2048,1536]{1,0:T(8,128)} %copy-done.8), kind=kOutput, calls=%fused_computation.18 | convolution fusion | flops 19355664384 | bytes 44040192 | tf_op jit(solution)/shard_map/bf,tbd->tfd/dot_general | solution.py:37
  233.3 21.8 %copy.21 = f32[4,1536,768]{2,0,1:T(4,128)} copy(f32[4,1536,768]{1,2,0:T(8,128)} %convolution_bitcast_fusion) | data formatting | bytes 37748736 | tf_op jit(solution)/shard_map/bf,tbd->tfd/transpose | solution.py:37
  255.1 29.1 %multiply_convert_fusion.clone.4 = bf16[4,2048,1536]{1,2,0:T(8,128)(2,1)} fusion(bf16[4,2048,768]{2,1,0:T(8,128)(2,1)} %copy-done.2, f32[2048,1536]{0,1:T(8,128)} %copy.18, bf16[1536,768]{1,0:T(8,128)(2,1)S(1)} %copy-done), kind=kOutput, calls=%fused_computation.4.clone.clone.clone.1 | convolution fusion | flops 19352518656 | bytes 52690944 | tf_op jit(solution)/shard_map/tbd,fd->tbf/dot_general | solution.py:38
  284.2 25.4 %convolution_bitcast_fusion.1 = f32[4,768,1536]{1,2,0:T(8,128)} fusion(bf16[2048,768]{1,0:T(8,128)(2,1)S(1)} %copy-done.3, bf16[4,2048,1536]{1,2,0:T(8,128)(2,1)} %multiply_convert_fusion.clone.4), kind=kOutput, calls=%fused_computation.19 | convolution fusion | flops 19327352832 | bytes 47185920 | tf_op jit(solution)/shard_map/bd,tbf->tdf/dot_general | solution.py:40
  309.7 22.8 %copy.19 = f32[4,768,1536]{2,0,1:T(4,128)} copy(f32[4,768,1536]{1,2,0:T(8,128)} %convolution_bitcast_fusion.1) | data formatting | bytes 37748736 | tf_op jit(solution)/shard_map/bd,tbf->tdf/transpose | solution.py:40
  335.0 434.6 %all-reduce.8.cloned.1.call-done = (f32[4,768,1536]{2,0,1:T(4,128)}, f32[4,1536,768]{2,0,1:T(4,128)}) async-done(((f32[4,768,1536]{2,0,1:T(4,128)}, f32[4,1536,768]{2,0,1:T(4,128)}), (f32[4,768,1536]{2,0,1:T(4,128)}, f32[4,1536,768]{2,0,1:T(4,128)})) %all-reduce.8.cloned.1.call-update) | async-done | bytes 37748752
  769.6 13.0 %fusion.29 = f32[4,4]{1,0:T(4,128)S(1)} fusion(f32[4,768,1536]{2,0,1:T(4,128)} %get-tuple-element.49, u32[]{:T(128)S(6)} %multiply.5), kind=kOutput, calls=%fused_computation.36 | convolution fusion | flops 28311552 | bytes 2359364 | tf_op jit(solution)/shard_map/tij,sij->ts/dot_general | solution.py:43
  782.6 13.6 %fusion.35 = f32[4,4]{1,0:T(4,128)S(1)} fusion(f32[4,4]{1,0:T(4,128)S(1)} %fusion.29, f32[4,1536,768]{2,0,1:T(4,128)} %get-tuple-element.50, u32[]{:T(128)S(6)} %multiply.7), kind=kOutput, calls=%fused_computation.40 | convolution fusion | flops 28311568 | bytes 2359428 | tf_op jit(solution)/shard_map/tij,sij->ts/dot_general | solution.py:44
  796.2 30.9 %psum.15 = f32[4,4]{1,0:T(4,128)S(1)} all-reduce(f32[4,4]{1,0:T(4,128)S(1)} %fusion.35), channel_id=1, replica_groups=mesh['model'=2,'data'=8] {'model','data'}, use_global_device_ids=true, to_apply=%region_5.6 | all-reduce | flops 16 | bytes 128 | tf_op jit(solution)/shard_map/psum | solution.py:45
  828.3 28.4 %while.11 = (s32[]{:T(128)}, f32[4]{0:T(128)S(1)}, f32[4,4]{1,0:T(4,128)S(1)}, f32[]{:T(128)}, s32[]{:T(128)}, /*index=5*/s32[]{:T(128)}) while((s32[]{:T(128)}, f32[4]{0:T(128)S(1)}, f32[4,4]{1,0:T(4,128)S(1)}, f32[]{:T(128)}, s32[]{:T(128)}, /*index=5*/s32[]{:T(128)}) %tuple.31), condition=%wide.region_10.11_spmd.clone, body=%wide.region_7.10_spmd.clone.sunk | while | flops 58 | bytes 300 | solution.py:17
  829.1 0.6 broadcast_divide_fusion.2
  830.5 0.6 broadcast_divide_fusion.2
  856.8 5.9 fusion.21
  862.7 5.9 fusion.25
  868.6 0.9 copy.31
  869.5 0.9 copy.32
  (103 shorter events, 28.9 us)
Async XLA Ops:
  7.2 19.6 %copy-start = (bf16[1536,768]{1,0:T(8,128)(2,1)S(1)}, bf16[1536,768]{1,0:T(8,128)(2,1)}, u32[]{:S(2)}) copy-start(bf16[1536,768]{1,0:T(8,128)(2,1)} %param.9) | copy-start | bytes 7077892
  7.2 179.7 %all-reduce.6.cloned.1.call-start = ((), (), s32[]{:S(2)}) async-start(), calls=%async_computation | async-start | bytes 12582912 | tf_op jit(solution)/shard_map/psum | solution.py:30
  22.2 4.6 copy-start.8
  35.9 733.7 %all-reduce.8.cloned.1.call-start = ((), (), s32[]{:S(2)}) async-start(), calls=%async_computation.1 | async-start | bytes 75497472
  36.4 150.5 %copy-start.4 = (bf16[4,768,3]{1,0,2:T(4,128)(2,1)S(1)}, bf16[4,768,3]{1,0,2:T(4,128)(2,1)}, u32[]{:S(2)}) copy-start(bf16[4,768,3]{1,0,2:T(4,128)(2,1)} %param.10) | copy-start | bytes 55300
  36.4 155.2 %copy-start.5 = (s32[4,2048]{1,0:T(4,128)S(1)}, s32[4,2048]{1,0:T(4,128)}, u32[]{:S(2)}) copy-start(s32[4,2048]{1,0:T(4,128)} %param.11) | copy-start | bytes 98308
  202.5 4.5 copy-start.2
  255.1 29.1 %copy-start.3 = (bf16[2048,768]{1,0:T(8,128)(2,1)S(1)}, bf16[2048,768]{1,0:T(8,128)(2,1)}, u32[]{:S(2)}) copy-start(bf16[2048,768]{1,0:T(8,128)(2,1)} %param.7) | copy-start | bytes 9437188
  332.5 0.7 copy-start.7
  332.5 537.8 %copy-start.1 = (bf16[1536,768]{1,0:T(8,128)(2,1)S(1)}, bf16[1536,768]{1,0:T(8,128)(2,1)}, u32[]{:S(2)}) copy-start(bf16[1536,768]{1,0:T(8,128)(2,1)} %param.9) | copy-start | bytes 7077892
  856.7 13.6 %copy-start.6 = (f32[4]{0:T(128)}, f32[4]{0:T(128)S(1)}, u32[]{:S(2)}) copy-start(f32[4]{0:T(128)S(1)} %get-tuple-element.22) | copy-start | bytes 52
Sparse Core Ops, SparseCore 0:
  36.0 150.8 all-reduce.5
  332.7 436.8 all-reduce.7
where the time goes:
time: 886 us; the launch traced here: 878 us
  waiting for transfers between devices  572 us (65%)
  matrix products  159 us (18%)
  local copies, waits for them, and re-layouts  69.2 us (8%)
  blocking collectives  30.9 us (3%)
  other arithmetic  28.4 us (3%)
  between operations  16.6 us (2%)
    unnamed x3, waiting for transfers between devices  435 us
    psum x1, waiting for transfers between devices, local_step(): mlp_out = lax.psum(part_out, 'model')  138 us
    psum x1, blocking collectives, local_step(): gram_mat = lax.psum(gram_part, ('model', 'data'))  30.9 us
    dot_general x1, matrix products, local_step(): jnp.einsum('tbd,fd->tbf', d_trunk, w_down, preferred_element_type=jnp.flo...  29.1 us
    dot_general x1, matrix products, local_step(): jnp.einsum('bf,tbd->tfd', act_bf, d_trunk, preferred_element_type=jnp.flo...  26.3 us
    dot_general x1, matrix products, local_step(): jnp.einsum('bd,tbf->tdf', tokens, d_pre, preferred_element_type=jnp.float32)  25.4 us
    transpose x1, local copies, waits for them, and re-layouts, local_step(): jnp.einsum('bd,tbf->tdf', tokens, d_pre, preferred_element_type=jnp.float32)  22.8 us
    transpose x1, local copies, waits for them, and re-layouts, local_step(): jnp.einsum('bf,tbd->tfd', act_bf, d_trunk, preferred_element_type=jnp.flo...  21.8 us
  transfers between devices with their start and end apart: 2, of which 2 were waited for; matrix products, arithmetic and copies ran while one was open for 2% of the time, Pallas kernels for 0%

commit v1 on v0

v1 whole, which is shorter than its diff:
```python
import functools

import jax
import jax.numpy as jnp
from jax import lax
from jax.experimental import pallas as pl
from jax.experimental.pallas import tpu as pltpu
from jax.sharding import PartitionSpec as P

STEPS = 20
MESH = pl.DeviceIdType.MESH
F32 = jnp.float32
BF16 = jnp.bfloat16
C0 = 0.7978845608028654
C1 = 0.044715
N_DATA = 8
N_TASK = 4
N_CLASS = 3
VMEM_LIMIT = 62 * 1024 * 1024


def gelu_only(a):
    return a * (0.5 + 0.5 * jnp.tanh(a * (C0 + (C0 * C1) * (a * a))))


def gelu_both(a):
    a2 = a * a
    t = jnp.tanh(a * (C0 + (C0 * C1) * a2))
    h = 0.5 + 0.5 * t
    slope = h + (0.5 * a) * (1.0 - t * t) * (C0 + (3.0 * C0 * C1) * a2)
    return a * h, slope


def nt_dot(a, b):
    return lax.dot_general(a, b, (((1,), (1,)), ((), ())), preferred_element_type=F32)


def nn_dot(a, b):
    return jnp.dot(a, b, preferred_element_type=F32)


def part_kernel(x_ref, w1_ref, w2_ref, out_ref):
    act = gelu_only(nn_dot(x_ref[...], w1_ref[...])).astype(BF16)
    out_ref[...] = nn_dot(act, w2_ref[...])


def part_call(x_half, w1, w2):
    rows, dim = x_half.shape
    ffn = w1.shape[1]
    blk = 256
    return pl.pallas_call(
        part_kernel,
        grid=(rows // blk,),
        out_shape=jax.ShapeDtypeStruct((rows, dim), F32),
        in_specs=[pl.BlockSpec((blk, dim), lambda i: (i, 0)),
                  pl.BlockSpec((dim, ffn), lambda i: (0, 0)),
                  pl.BlockSpec((ffn, dim), lambda i: (0, 0))],
        out_specs=pl.BlockSpec((blk, dim), lambda i: (i, 0)),
        compiler_params=pltpu.CompilerParams(vmem_limit_bytes=VMEM_LIMIT),
        cost_estimate=pl.CostEstimate(flops=4 * rows * dim * ffn, bytes_accessed=12_000_000, transcendentals=0),
    )(x_half, w1, w2)


def err_kernel(n_total, x_ref, w1_ref, w2_ref, part_ref, lab_ref, head_ref, out_ref, own_ref, send_sem, recv_sem, loc_sem):
    i = pl.program_id(0)
    blk = x_ref.shape[0]
    m = lax.axis_index('model')
    d = lax.axis_index('data')
    offs = [(dz, dr) for dz in (0, 1) for dr in range(4) if dz or dr]

    @pl.when(i == 0)
    def _():
        barrier = pltpu.get_barrier_semaphore()
        for dz, dr in offs:
            dev = (lax.rem(m + dz, 2), xor_data(d, dr))
            pl.semaphore_signal(barrier, inc=1, device_id=dev, device_id_type=MESH)
        pl.semaphore_wait(barrier, len(offs))

    x = x_ref[...]
    act = gelu_only(nn_dot(x, w1_ref[...])).astype(BF16)
    mlp = part_ref[...] + nn_dot(act, w2_ref[...])
    z = (x.astype(F32) + mlp).astype(BF16)
    logits = nt_dot(head_ref[...], z)
    lg = [logits[8 * c:8 * c + 8, :] for c in range(N_CLASS)]
    top = jnp.maximum(jnp.maximum(lg[0], lg[1]), lg[2])
    ex = [jnp.exp(v - top) for v in lg]
    tot = ex[0] + ex[1] + ex[2]
    lab = lab_ref[...]
    col = pl.ds(pl.multiple_of(i * blk, blk), blk)
    errs = []
    for c in range(N_CLASS):
        hot = jnp.where(lab == c, 1.0, 0.0)
        errs.append((ex[c] / tot - hot) * (1.0 / n_total))
    for c in range(N_CLASS):
        own_ref[8 * c:8 * c + 8, col] = errs[c]

    @pl.when(i == pl.num_programs(0) - 1)
    def _():
        loc = pltpu.make_async_copy(own_ref, out_ref.at[0, m], loc_sem)
        loc.start()
        copies = []
        for k, (dz, dr) in enumerate(offs):
            dev = (lax.rem(m + dz, 2), xor_data(d, dr))
            copies.append(pltpu.make_async_remote_copy(
                own_ref, out_ref.at[dr, m], send_sem.at[k], recv_sem.at[k], device_id=dev, device_id_type=MESH))
            copies[-1].start()
        for cp in copies:
            cp.wait()
        loc.wait()


def xor_data(d, dr):
    core = lax.rem(d, 2)
    x = lax.rem(d // 2, 2)
    y = d // 4
    return (lax.rem(y + dr // 2, 2) * 2 + lax.rem(x + dr % 2, 2)) * 2 + core


def err_call(n_total, x_half, w1, w2, part, lab8, heads24):
    rows, dim = x_half.shape
    ffn = w1.shape[1]
    blk = 256
    return pl.pallas_call(
        functools.partial(err_kernel, n_total),
        grid=(rows // blk,),
        out_shape=jax.ShapeDtypeStruct((4, 2, 24, rows), F32),
        in_specs=[pl.BlockSpec((blk, dim), lambda i: (i, 0)),
                  pl.BlockSpec((dim, ffn), lambda i: (0, 0)),
                  pl.BlockSpec((ffn, dim), lambda i: (0, 0)),
                  pl.BlockSpec((blk, dim), lambda i: (i, 0)),
                  pl.BlockSpec((8, blk), lambda i: (0, i)),
                  pl.BlockSpec((24, dim), lambda i: (0, 0))],
        out_specs=pl.BlockSpec(memory_space=pl.ANY),
        scratch_shapes=[pltpu.VMEM((24, rows), F32),
                        pltpu.SemaphoreType.DMA((7,)), pltpu.SemaphoreType.DMA((7,)), pltpu.SemaphoreType.DMA],
        compiler_params=pltpu.CompilerParams(vmem_limit_bytes=VMEM_LIMIT, collective_id=0, has_side_effects=True),
        cost_estimate=pl.CostEstimate(flops=4 * rows * dim * ffn, bytes_accessed=12_000_000, transcendentals=0),
    )(x_half, w1, w2, part, lab8, heads24)


def grad_body(x_ref, e_ref, w1t_ref, w2s_ref, hb_ref, g1_ref, g2_ref, dz_ref, da_ref, ut_ref, sl_ref, first):
    blk, dim = x_ref.shape
    sl = w1t_ref.shape[0]
    pre = nt_dot(w1t_ref[...], x_ref[...])
    act, slope = gelu_both(pre)
    ut_ref[...] = act.astype(BF16)
    sl_ref[...] = slope
    rows = 32
    for t in range(N_TASK):
        slot = t % 2
        es = [[e_ref[8 * c + t:8 * c + t + 1, 128 * j:128 * j + 128] for j in range(blk // 128)] for c in range(N_CLASS)]
        for r0 in range(0, dim, rows):
            h = [hb_ref[N_CLASS * t + c, r0:r0 + rows, :] for c in range(N_CLASS)]
            for j in range(blk // 128):
                val = h[0] * es[0][j] + h[1] * es[1][j] + h[2] * es[2][j]
                dz_ref[slot, r0:r0 + rows, 128 * j:128 * j + 128] = val.astype(BF16)
        da = nn_dot(w2s_ref[...], dz_ref[slot])
        da_ref[slot] = (da * sl_ref[...]).astype(BF16)
        g2 = nt_dot(ut_ref[...], dz_ref[slot])
        g1 = nn_dot(da_ref[slot], x_ref[...])
        out = pl.ds(t * sl, sl)
        if first:
            g2_ref[out, :] = g2
            g1_ref[out, :] = g1
        else:
            g2_ref[out, :] += g2
            g1_ref[out, :] += g1


def grad_kernel(has_acc, x_ref, e_ref, w1t_ref, w2s_ref, hb_ref, *rest):
    if has_acc:
        g1_in, g2_in, g1_ref, g2_ref, dz_ref, da_ref, ut_ref, sl_ref = rest
    else:
        g1_ref, g2_ref, dz_ref, da_ref, ut_ref, sl_ref = rest

    @pl.when(pl.program_id(0) == 0)
    def _():
        if has_acc:
            g1_ref[...] = g1_in[...]
            g2_ref[...] = g2_in[...]
        else:
            g1_ref[...] = jnp.zeros_like(g1_ref)
            g2_ref[...] = jnp.zeros_like(g2_ref)

    grad_body(x_ref, e_ref.at[0, 0], w1t_ref, w2s_ref, hb_ref, g1_ref, g2_ref, dz_ref, da_ref, ut_ref, sl_ref, False)


def grad_call(x_set, errs, rel, w1t, w2s, hb, acc):
    rows, dim = x_set.shape
    sl = w1t.shape[0]
    blk = 512
    per = errs.shape[3] // blk
    acc_spec = pl.BlockSpec((N_TASK * sl, dim), lambda i: (0, 0))
    acc_shape = jax.ShapeDtypeStruct((N_TASK * sl, dim), F32)
    in_specs = [pl.BlockSpec((blk, dim), lambda i: (i, 0)),
                pl.BlockSpec((1, 1, 24, blk), lambda i: (rel, i // per, 0, lax.rem(i, per))),
                pl.BlockSpec((sl, dim), lambda i: (0, 0)),
                pl.BlockSpec((sl, dim), lambda i: (0, 0)),
                pl.BlockSpec(hb.shape, lambda i: (0, 0, 0))]
    args = [x_set, errs, w1t, w2s, hb]
    if acc is not None:
        in_specs += [acc_spec, acc_spec]
        args += list(acc)
    return pl.pallas_call(
        functools.partial(grad_kernel, acc is not None),
        grid=(rows // blk,),
        out_shape=[acc_shape, acc_shape],
        in_specs=in_specs,
        out_specs=[acc_spec, acc_spec],
        scratch_shapes=[pltpu.VMEM((2, dim, blk), BF16), pltpu.VMEM((2, sl, blk), BF16),
                        pltpu.VMEM((sl, blk), BF16), pltpu.VMEM((sl, blk), F32)],
        compiler_params=pltpu.CompilerParams(vmem_limit_bytes=VMEM_LIMIT),
        cost_estimate=pl.CostEstimate(flops=26 * rows * dim * sl, bytes_accessed=30_000_000, transcendentals=0),
    )(*args)


def tail_kernel(g1_ref, g2_ref, wts_ref, out1_ref, out2_ref, rx1, rx2, gr_own, gr_all, tr_ref, rx_g1,
                half_send, half_recv, gram_send, gram_recv, out_send, out_recv, loc_sem):
    m = lax.axis_index('model')
    d = lax.axis_index('data')
    core = lax.rem(d, 2)
    n_data = N_DATA
    half = rx1.shape[1]
    sl = 2 * half
    dim = g1_ref.shape[1]
    me = m * n_data + d

    barrier = pltpu.get_barrier_semaphore()
    for k in range(1, 2 * n_data):
        p = lax.rem(me + k, 2 * n_data)
        pl.semaphore_signal(barrier, inc=1, device_id=(p // n_data, lax.rem(p, n_data)), device_id_type=MESH)
    pl.semaphore_wait(barrier, 2 * n_data - 1)

    peer = (m, d + 1 - 2 * core)
    keep = pl.multiple_of(core * half, half)
    give = pl.multiple_of((1 - core) * half, half)
    copies = []
    for a, (src, dst) in enumerate(((g1_ref, rx1), (g2_ref, rx2))):
        for t in range(N_TASK):
            copies.append(pltpu.make_async_remote_copy(
                src.at[pl.ds(t * sl + give, half), :], dst.at[t], half_send.at[a, t], half_recv.at[a, t],
                device_id=peer, device_id_type=MESH))
            copies[-1].start()
    pairs = [(i, j) for i in range(N_TASK) for j in range(i, N_TASK)]
    acc = tuple(jnp.zeros((8, 128), F32) for _ in pairs)
    for a, (src, dst) in enumerate(((g1_ref, rx1), (g2_ref, rx2))):
        for cp in copies[a * N_TASK:(a + 1) * N_TASK]:
            cp.wait_recv()

        def fold(r, acc):
            row = pl.multiple_of(r * 8, 8)
            acc = list(acc)
            for l in range(0, dim, 128):
                gs = []
                for t in range(N_TASK):
                    v = dst[t, pl.ds(row, 8), l:l + 128] + src[pl.ds(pl.multiple_of(t * sl + keep + row, 8), 8), l:l + 128]
                    dst[t, pl.ds(row, 8), l:l + 128] = v
                    gs.append(v)
                for q, (i, j) in enumerate(pairs):
                    acc[q] = acc[q] + gs[i] * gs[j]
            return tuple(acc)

        acc = lax.fori_loop(0, half // 8, fold, acc)
    for cp in copies:
        cp.wait_send()
    gr_own[...] = jnp.zeros_like(gr_own)
    for q in range(len(pairs)):
        gr_own[q:q + 1, :] = jnp.sum(acc[q], axis=0, keepdims=True)
    loc = pltpu.make_async_copy(gr_own, gr_all.at[me], loc_sem)
    loc.start()
    gcopies = []
    for k in range(1, 2 * n_data):
        p = lax.rem(me + k, 2 * n_data)
        gcopies.append(pltpu.make_async_remote_copy(
            gr_own, gr_all.at[me], gram_send.at[k - 1], gram_recv.at[k - 1],
            device_id=(p // n_data, lax.rem(p, n_data)), device_id_type=MESH))
        gcopies[-1].start()
    for cp in gcopies:
        cp.wait()
    loc.wait()
    tot = gr_all[0]
    for k in range(1, 2 * n_data):
        tot = tot + gr_all[k]
    sums = jnp.broadcast_to(jnp.sum(tot, axis=1, keepdims=True), tot.shape)
    gram = {}
    for q, (i, j) in enumerate(pairs):
        gram[i, j] = gram[j, i] = sums[q:q + 1, :]
    scale = (gram[0, 0] + gram[1, 1] + gram[2, 2] + gram[3, 3]) / N_TASK

    def eg_step(k, w):
        up = []
        for i in range(N_TASK):
            mv = gram[i, 0] * w[0] + gram[i, 1] * w[1] + gram[i, 2] * w[2] + gram[i, 3] * w[3]
            up.append(w[i] * jnp.exp(-mv / scale))
        s = up[0] + up[1] + up[2] + up[3]
        return tuple(u / s for u in up)

    w = lax.fori_loop(0, STEPS, eg_step, tuple(jnp.full((1, 128), 1.0 / N_TASK, F32) for _ in range(N_TASK)))
    wts_ref[...] = jnp.zeros_like(wts_ref)
    for t in range(N_TASK):
        wts_ref[t:t + 1, :] = w[t]
    w1 = [jnp.broadcast_to(v, (half, 128)) for v in w]
    for l in range(0, dim, 128):
        v = w1[0] * rx1[0, :, l:l + 128]
        for t in range(1, N_TASK):
            v = v + w1[t] * rx1[t, :, l:l + 128]
        tr_ref[l:l + 128, 0:half] = v.T
    per = dim // n_data
    ocopies = []
    for k in range(1, n_data):
        p = lax.rem(d + k, n_data)
        ocopies.append(pltpu.make_async_remote_copy(
            tr_ref.at[pl.ds(pl.multiple_of(p * per, per), per), :], rx_g1.at[d], out_send.at[k - 1], out_recv.at[k - 1],
            device_id=(m, p), device_id_type=MESH))
        ocopies[-1].start()
    loc = pltpu.make_async_copy(tr_ref.at[pl.ds(pl.multiple_of(d * per, per), per), :], rx_g1.at[d], loc_sem)
    loc.start()
    for l in range(0, dim, 128):
        v = w1[0] * rx2[0, :, l:l + 128]
        for t in range(1, N_TASK):
            v = v + w1[t] * rx2[t, :, l:l + 128]
        out2_ref[:, l:l + 128] = v
    loc.wait()
    for cp in ocopies:
        cp.wait()
    for k in range(n_data):
        out1_ref[:, k * half:(k + 1) * half] = rx_g1[k, :, 0:half]


def tail_call(g1, g2):
    rows, dim = g1.shape
    sl = rows // N_TASK
    half = sl // 2
    per = dim // N_DATA
    n_dev = 2 * N_DATA
    vm = pl.BlockSpec(memory_space=pltpu.VMEM)
    return pl.pallas_call(
        tail_kernel,
        out_shape=[jax.ShapeDtypeStruct((8, 128), F32), jax.ShapeDtypeStruct((per, half * N_DATA), F32),
                   jax.ShapeDtypeStruct((half, dim), F32)],
        in_specs=[vm, vm],
        out_specs=[vm, vm, vm],
        scratch_shapes=[pltpu.VMEM((N_TASK, half, dim), F32), pltpu.VMEM((N_TASK, half, dim), F32),
                        pltpu.VMEM((16, 128), F32), pltpu.VMEM((n_dev, 16, 128), F32),
                        pltpu.VMEM((dim, 256), F32), pltpu.VMEM((N_DATA, per, 256), F32),
                        pltpu.SemaphoreType.DMA((2, N_TASK)), pltpu.SemaphoreType.DMA((2, N_TASK)),
                        pltpu.SemaphoreType.DMA((n_dev - 1,)), pltpu.SemaphoreType.DMA((n_dev - 1,)),
                        pltpu.SemaphoreType.DMA((N_DATA - 1,)), pltpu.SemaphoreType.DMA((N_DATA - 1,)),
                        pltpu.SemaphoreType.DMA],
        compiler_params=pltpu.CompilerParams(vmem_limit_bytes=VMEM_LIMIT, collective_id=1, has_side_effects=True),
    )(g1, g2)


def swap(v, bit):
    return lax.ppermute(v, 'data', [(i, i ^ bit) for i in range(N_DATA)])


def solution(mesh):
    n_data = mesh.shape['data']

    def local_step(tokens, w_up, w_down, task_heads, labels):
        m = lax.axis_index('model')
        d = lax.axis_index('data')
        n_loc, dim = tokens.shape
        n_total = n_loc * n_data
        n_half = n_loc // 2
        wide = w_up.shape[1]
        sl = 2 * wide // n_data
        flip = [(0, 1), (1, 0)]
        p1 = dim // n_data
        p2 = wide // n_data
        w1_part = lax.ppermute(lax.dynamic_slice_in_dim(w_up, d * p1, p1, 0), 'model', flip)
        w2_part = lax.ppermute(lax.dynamic_slice_in_dim(w_down, d * p2, p2, 0), 'model', flip)
        w1_far = lax.all_gather(w1_part, 'data', axis=0, tiled=True)
        w2_far = lax.all_gather(w2_part, 'data', axis=0, tiled=True)
        x_a = swap(tokens, 2)
        x_b = swap(tokens, 4)
        x_c0 = swap(x_a[:n_half], 4)
        x_c1 = swap(x_b[n_half:], 2)

        heads_t = task_heads.transpose(2, 0, 1)
        heads24 = jnp.pad(heads_t, ((0, 0), (0, 4), (0, 0))).reshape(24, dim)
        hb = jnp.broadcast_to(task_heads.astype(F32).transpose(0, 2, 1).reshape(12, dim, 1), (12, dim, 128))
        chip = d // 2
        w1t = lax.dynamic_slice_in_dim(w_up, chip * sl, sl, 1).T
        w2s = lax.dynamic_slice_in_dim(w_down, chip * sl, sl, 0)
        x_half = lax.dynamic_slice_in_dim(tokens, m * n_half, n_half, 0)
        lab8 = jnp.pad(lax.dynamic_slice_in_dim(labels, m * n_half, n_half, 1), ((0, 4), (0, 0)))

        part = part_call(x_half, w_up, w_down)
        errs = err_call(n_total, x_half, w1_far, w2_far, part, lab8, heads24)
        acc = grad_call(tokens, errs, 0, w1t, w2s, hb, None)
        acc = grad_call(x_a, errs, 1, w1t, w2s, hb, acc)
        acc = grad_call(x_b, errs, 2, w1t, w2s, hb, acc)
        x_c = jnp.concatenate([x_c0, x_c1], axis=0)
        acc = grad_call(x_c, errs, 3, w1t, w2s, hb, acc)
        wts, grad_up, grad_down = tail_call(*acc)
        return wts[:N_TASK, 0], grad_up, grad_down

    return jax.shard_map(
        local_step, mesh=mesh,
        in_specs=(P('data', None), P(None, 'model'), P('model', None), P(None, None, None), P(None, 'data')),
        out_specs=(P(None), P('data', 'model'), P(('model', 'data'), None)),
        check_vma=False)
```

time: 886 us -> 335 us (0.38)
  waiting for transfers between devices: 572 us -> 79.8 us
  Pallas kernels: 0 us -> 206 us
  matrix products: 159 us -> 0 us
  local copies, waits for them, and re-layouts: 69.2 us -> 24.1 us
  blocking collectives: 30.9 us -> 0 us
  other arithmetic: 28.4 us -> 3.81 us
    unnamed x3 -> x2, waiting for transfers between devices: 435 us -> 0.03 us
    pallas_call x0 -> x7, Pallas kernels: none -> 206 us  [the longest x4 119 us: grad_call(): pl.pallas_call(functools.partial(grad_kernel, acc is not None), grid=(row...]
    dot_general x11 -> x0, matrix products: 159 us -> none  [the longest x1 29.1 us: local_step(): jnp.einsum('tbd,fd->tbf', d_trunk, w_down, preferred_element_type=jnp.flo...]
    psum x1 -> x0, waiting for transfers between devices: 138 us -> none  [local_step(): mlp_out = lax.psum(part_out, 'model')]
    ppermute x0 -> x6, waiting for transfers between devices: none -> 79.7 us  [the longest x4 66.9 us: swap(): return lax.ppermute(v, 'data', [(i, i ^ bit) for i in range(N_DATA)])]
    transpose x2 -> x0, local copies, waits for them, and re-layouts: 44.7 us -> none  [the longest x1 22.8 us: local_step(): jnp.einsum('bd,tbf->tdf', tokens, d_pre, preferred_element_type=jnp.float32)]
    psum x1 -> x0, blocking collectives: 30.9 us -> none  [local_step(): gram_mat = lax.psum(gram_part, ('model', 'data'))]
    reduce_sum x42 -> x0, other arithmetic: 15.3 us -> none  [the longest x20 12.4 us: eg_step(): return updated / jnp.sum(updated)]
  transfers between devices with their start and end apart: 2 -> 8, of which waited for: 2 -> 3; matrix products, arithmetic and copies ran while one was open for 2% -> 5% of each run, Pallas kernels for 0% -> 42%
where the time goes in v1:
time: 335 us; the launch traced here: 334 us
  Pallas kernels  206 us (61%)
  waiting for transfers between devices  79.8 us (24%)
  local copies, waits for them, and re-layouts  24.1 us (7%)
  between operations  14.1 us (4%)
  starting transfers between devices  6.71 us (2%)
  other arithmetic  3.81 us (1%)
    pallas_call x4, Pallas kernels, grad_call(): pl.pallas_call(functools.partial(grad_kernel, acc is not None), grid=(row...  119 us
    ppermute x4, waiting for transfers between devices, swap(): return lax.ppermute(v, 'data', [(i, i ^ bit) for i in range(N_DATA)])  66.9 us
    pallas_call x1, Pallas kernels, err_call(): pl.pallas_call(functools.partial(err_kernel, n_total), grid=(rows // blk,...  43.5 us
    pallas_call x1, Pallas kernels, tail_call(): pl.pallas_call(tail_kernel, out_shape=[jax.ShapeDtypeStruct((8, 128), F32...  33.7 us
    pallas_call x1, Pallas kernels, part_call(): pl.pallas_call(part_kernel, grid=(rows // blk,), out_shape=jax.ShapeDtype...  9.64 us
    ppermute x1, waiting for transfers between devices, local_step(): lax.ppermute(lax.dynamic_slice_in_dim(w_up, d * p1, p1, 0), 'model', flip)  6.71 us
  transfers between devices with their start and end apart: 8, of which 3 were waited for; matrix products, arithmetic and copies ran while one was open for 5% of the time, Pallas kernels for 42%

profile of v1, /device:TPU:1, one launch (start us, length us, event | category | flops | bytes accessed | tf_op | source)
XLA Modules:
  0.0 334.3 jit_solution(7068779832939616355)
XLA Ops:
  8.2 2.2 collective-permute-start.4
  10.4 6.7 %collective-permute-done.4 = bf16[96,1536]{1,0:T(8,128)(2,1)S(1)} collective-permute-done((bf16[96,1536]{1,0:T(8,128)(2,1)S(1)}, bf16[96,1536]{1,0:T(8,128)(2,1)S(1)}, u32[]{:S(2)}, u32[]{:S(2)}) %collective-permute-start.4) | collective-permute-done | bytes 294944 | tf_op jit(solution)/shard_map/ppermute | solution.py:372
  18.9 1.2 collective-permute-start.5
  20.1 6.1 %collective-permute-done.5 = bf16[192,768]{1,0:T(8,128)(2,1)S(1)} collective-permute-done((bf16[192,768]{1,0:T(8,128)(2,1)S(1)}, bf16[192,768]{1,0:T(8,128)(2,1)S(1)}, u32[]{:S(2)}, u32[]{:S(2)}) %collective-permute-start.5) | collective-permute-done | bytes 294944 | tf_op jit(solution)/shard_map/ppermute | solution.py:373
  27.8 1.2 collective-permute-start.2
  29.0 1.1 constant_dynamic-slice_fusion.1
  32.5 1.9 constant_dynamic-slice_fusion.w2s_ref
  34.5 2.7 constant_dynamic-slice_fusion.5.x_ref
  37.2 9.6 %shard_map.76.part_ref = f32[1024,768]{1,0:T(8,128)} custom-call(bf16[1024,768]{1,0:T(8,128)(2,1)} %constant_dynamic-slice_fusion.5.x_ref, bf16[768,1536]{1,0:T(8,128)(2,1)} %w1_ref.1, bf16[1536,768]{1,0:T(8,128)(2,1)} %w2_ref.1), custom_call_target="tpu_custom_call" | custom-call | flops 4831838208 | bytes 12000000 | tf_op jit(solution)/shard_map/pallas_call | solution.py:51
  46.8 66.9 %collective-permute-done.x_ref = bf16[2048,768]{1,0:T(8,128)(2,1)} collective-permute-done((bf16[2048,768]{1,0:T(8,128)(2,1)}, bf16[2048,768]{1,0:T(8,128)(2,1)}, u32[]{:S(2)}, u32[]{:S(2)}) %collective-permute-start) | collective-permute-done | bytes 3145760 | tf_op jit(solution)/shard_map/ppermute | solution.py:355
  113.7 1.5 slice.12
  115.2 1.2 collective-permute-start.1
  116.4 2.7 slice.13
  119.1 43.5 %shard_map.77.e_ref = f32[4,2,24,1024]{3,2,1,0:T(8,128)} custom-call(bf16[1024,768]{1,0:T(8,128)(2,1)} %constant_dynamic-slice_fusion.5.x_ref, bf16[768,1536]{1,0:T(8,128)(2,1)} %all-gather.3.cloned.1.call-done.w1_ref, bf16[1536,768]{1,0:T(8,128)(2,1)} %all-gather.5.cloned.1.call-done.w2_ref, f32[1024,768]{1,0:T(8,128)} %shard_map.76.part_ref, ...), custom_call_target="tpu_custom_call" | custom-call | flops 4831838208 | bytes 12000000 | tf_op jit(solution)/shard_map/pallas_call | solution.py:123
  162.5 3.3 broadcast_in_dim.12.hb_ref
  165.8 27.7 %shard_map.78 = (f32[1536,768]{1,0:T(8,128)}, f32[1536,768]{1,0:T(8,128)}) custom-call(bf16[2048,768]{1,0:T(8,128)(2,1)} %x_ref.1, f32[4,2,24,1024]{3,2,1,0:T(8,128)} %shard_map.77.e_ref, bf16[384,768]{1,0:T(8,128)(2,1)} %bitcast.6, bf16[384,768]{1,0:T(8,128)(2,1)} %constant_dynamic-slice_fusion.w2s_ref, f32[12,768,128]{2,1,0:T(8,128)} %broadcast_in_dim.12.hb_ref), custom_call_target="tpu_custom_call" | custom-call | flops 15703474176 | bytes 30000000 | tf_op jit(solution)/shard_map/pallas_call | solution.py:204
  193.5 30.5 %shard_map.79 = (f32[1536,768]{1,0:T(8,128)}, f32[1536,768]{1,0:T(8,128)}) custom-call(bf16[2048,768]{1,0:T(8,128)(2,1)} %collective-permute-done.x_ref, f32[4,2,24,1024]{3,2,1,0:T(8,128)} %shard_map.77.e_ref, bf16[384,768]{1,0:T(8,128)(2,1)} %bitcast.7, bf16[384,768]{1,0:T(8,128)(2,1)} %constant_dynamic-slice_fusion.w2s_ref, ...), custom_call_target="tpu_custom_call" | custom-call | flops 15703474176 | bytes 30000000 | tf_op jit(solution)/shard_map/pallas_call | solution.py:204
  224.1 30.4 %shard_map.80 = (f32[1536,768]{1,0:T(8,128)}, f32[1536,768]{1,0:T(8,128)}) custom-call(bf16[2048,768]{1,0:T(8,128)(2,1)} %collective-permute-done.2.x_ref, f32[4,2,24,1024]{3,2,1,0:T(8,128)} %shard_map.77.e_ref, bf16[384,768]{1,0:T(8,128)(2,1)} %bitcast.8, bf16[384,768]{1,0:T(8,128)(2,1)} %constant_dynamic-slice_fusion.w2s_ref, ...), custom_call_target="tpu_custom_call" | custom-call | flops 15703474176 | bytes 30000000 | tf_op jit(solution)/shard_map/pallas_call | solution.py:204
  254.5 3.8 %pad_maximum_fusion.x_ref = bf16[2048,768]{1,0:T(8,128)(2,1)} fusion(bf16[1024,768]{1,0:T(8,128)(2,1)} %collective-permute-done.3, bf16[1024,768]{1,0:T(8,128)(2,1)} %collective-permute-done.1), kind=kLoop, calls=%fused_computation | loop fusion | flops 6291456 | bytes 6291456 | tf_op jit(solution)/shard_map/concatenate | solution.py:395
  258.3 30.3 %shard_map.81 = (f32[1536,768]{1,0:T(8,128)}, f32[1536,768]{1,0:T(8,128)}) custom-call(bf16[2048,768]{1,0:T(8,128)(2,1)} %pad_maximum_fusion.x_ref, f32[4,2,24,1024]{3,2,1,0:T(8,128)} %shard_map.77.e_ref, bf16[384,768]{1,0:T(8,128)(2,1)} %bitcast.9, bf16[384,768]{1,0:T(8,128)(2,1)} %constant_dynamic-slice_fusion.w2s_ref, ...), custom_call_target="tpu_custom_call" | custom-call | flops 15703474176 | bytes 30000000 | tf_op jit(solution)/shard_map/pallas_call | solution.py:204
  288.6 33.7 %shard_map.82 = (f32[8,128]{1,0:T(8,128)}, f32[96,1536]{1,0:T(8,128)}, f32[192,768]{1,0:T(8,128)}) custom-call(f32[1536,768]{1,0:T(8,128)} %get-tuple-element.20.g1_ref, f32[1536,768]{1,0:T(8,128)} %get-tuple-element.21.g2_ref), custom_call_target="tpu_custom_call" | custom-call | tf_op jit(solution)/shard_map/pallas_call | solution.py:337
  322.3 1.3 slice_reduce_fusion
  323.6 1.9 copy.14
  325.5 1.9 copy.15
  (30 shorter events, 6.7 us)
Async XLA Ops:
  7.2 24.1 %copy-start = (s32[4,2048]{1,0:T(4,128)S(1)}, s32[4,2048]{1,0:T(4,128)}, u32[]{:S(2)}) copy-start(s32[4,2048]{1,0:T(4,128)} %param.9) | copy-start | bytes 98308
  7.2 24.7 %copy-start.4 = (bf16[4,768,3]{1,0,2:T(4,128)(2,1)S(1)}, bf16[4,768,3]{1,0,2:T(4,128)(2,1)}, u32[]{:S(2)}) copy-start(bf16[4,768,3]{1,0,2:T(4,128)(2,1)} %param.8) | copy-start | bytes 55300
  7.2 111.9 %all-gather.3.cloned.1.call-start = ((), (), s32[]{:S(2)}) async-start(), calls=%async_computation | async-start | bytes 2654208 | tf_op jit(solution)/shard_map/all_gather | solution.py:374
  8.2 8.9 %collective-permute-start.4 = (bf16[96,1536]{1,0:T(8,128)(2,1)S(1)}, bf16[96,1536]{1,0:T(8,128)(2,1)S(1)}, u32[]{:S(2)}, u32[]{:S(2)}) collective-permute-start(bf16[96,1536]{1,0:T(8,128)(2,1)S(1)} %constant_dynamic-slice_fusion.4), channel_id=1, source_target_pairs={{0,8},{8,0},{1,9},{9,1},{2,10},{10,2},{3,11},{11,3},{4,12},{12,4},... | collective-permute-start | bytes 884744 | tf_op jit(solution)/shard_map/ppermute | solution.py:372
  17.1 0.7 copy-start.2
  17.8 101.2 %all-gather.5.cloned.1.call-start = ((), (), s32[]{:S(2)}) async-start(), calls=%async_computation.1 | async-start | bytes 2654208 | tf_op jit(solution)/shard_map/all_gather | solution.py:375
  18.9 7.4 %collective-permute-start.5 = (bf16[192,768]{1,0:T(8,128)(2,1)S(1)}, bf16[192,768]{1,0:T(8,128)(2,1)S(1)}, u32[]{:S(2)}, u32[]{:S(2)}) collective-permute-start(bf16[192,768]{1,0:T(8,128)(2,1)S(1)} %constant_dynamic-slice_fusion.3), channel_id=1, source_target_pairs={{0,8},{8,0},{1,9},{9,1},{2,10},{10,2},{3,11},{11,3},{4,12},{12,4},... | collective-permute-start | bytes 884744 | tf_op jit(solution)/shard_map/ppermute | solution.py:373
  26.2 0.7 copy-start.3
  27.0 86.8 %collective-permute-start = (bf16[2048,768]{1,0:T(8,128)(2,1)}, bf16[2048,768]{1,0:T(8,128)(2,1)}, u32[]{:S(2)}, u32[]{:S(2)}) collective-permute-start(bf16[2048,768]{1,0:T(8,128)(2,1)} %x_ref.1), channel_id=1, source_target_pairs={{0,2},{1,3},{2,0},{3,1},{4,6},{5,7},{6,4},{7,5},{8,10},{9,11},{10,... | collective-permute-start | bytes 9437192 | tf_op jit(solution)/shard_map/ppermute | solution.py:355
  27.8 88.6 %collective-permute-start.2 = (bf16[2048,768]{1,0:T(8,128)(2,1)}, bf16[2048,768]{1,0:T(8,128)(2,1)}, u32[]{:S(2)}, u32[]{:S(2)}) collective-permute-start(bf16[2048,768]{1,0:T(8,128)(2,1)} %x_ref.1), channel_id=1, source_target_pairs={{0,4},{1,5},{2,6},{3,7},{4,0},{5,1},{6,2},{7,3},{8,12},{9,13},{10,... | collective-permute-start | bytes 9437192 | tf_op jit(solution)/shard_map/ppermute | solution.py:355
  115.2 139.2 %collective-permute-start.1 = (bf16[1024,768]{1,0:T(8,128)(2,1)S(1)}, bf16[1024,768]{1,0:T(8,128)(2,1)}, u32[]{:S(2)}, u32[]{:S(2)}) collective-permute-start(bf16[1024,768]{1,0:T(8,128)(2,1)S(1)} %slice.12), channel_id=1, source_target_pairs={{0,4},{1,5},{2,6},{3,7},{4,0},{5,1},{6,2},{7,3},{8,12},{9,13},{10,... | collective-permute-start | bytes 4718600 | tf_op jit(solution)/shard_map/ppermute | solution.py:355
  119.1 135.4 %collective-permute-start.3 = (bf16[1024,768]{1,0:T(8,128)(2,1)}, bf16[1024,768]{1,0:T(8,128)(2,1)}, u32[]{:S(2)}, u32[]{:S(2)}) collective-permute-start(bf16[1024,768]{1,0:T(8,128)(2,1)} %slice.13), channel_id=1, source_target_pairs={{0,2},{1,3},{2,0},{3,1},{4,6},{5,7},{6,4},{7,5},{8,10},{9,11},{10,... | collective-permute-start | bytes 4718600 | tf_op jit(solution)/shard_map/ppermute | solution.py:355
  288.6 38.9 %copy-start.1 = (s32[4,2048]{1,0:T(4,128)S(1)}, s32[4,2048]{1,0:T(4,128)}, u32[]{:S(2)}) copy-start(s32[4,2048]{1,0:T(4,128)} %param.9) | copy-start | bytes 98308
Sparse Core Ops, SparseCore 0:
  18.0 34.9 all-gather.2
  54.8 35.0 all-gather.4

commit v2 on v0

v2 whole, which is shorter than its diff:
```python
import functools

import jax
import jax.numpy as jnp
from jax import lax
from jax.experimental import pallas as pl
from jax.experimental.pallas import tpu as pltpu
from jax.sharding import PartitionSpec as P

STEPS = 20
MESH = pl.DeviceIdType.MESH
F32 = jnp.float32
BF16 = jnp.bfloat16
C0 = 0.7978845608028654
C1 = 0.044715
N_DATA = 8
N_DEV = 16
N_TASK = 4
N_CLASS = 3
BLK = 512
VMEM_LIMIT = 63 * 1024 * 1024


def gelu_only(a):
    return a * (0.5 + 0.5 * jnp.tanh(a * (C0 + (C0 * C1) * (a * a))))


def gelu_both(a):
    a2 = a * a
    t = jnp.tanh(a * (C0 + (C0 * C1) * a2))
    h = 0.5 + 0.5 * t
    slope = h + (0.5 * a) * (1.0 - t * t) * (C0 + (3.0 * C0 * C1) * a2)
    return a * h, slope


def nt_dot(a, b):
    return lax.dot_general(a, b, (((1,), (1,)), ((), ())), preferred_element_type=F32)


def nn_dot(a, b):
    return jnp.dot(a, b, preferred_element_type=F32)


def xor_data(d, dr):
    core = lax.rem(d, 2)
    x = lax.rem(d // 2, 2)
    y = d // 4
    return (lax.rem(y + dr // 2, 2) * 2 + lax.rem(x + dr % 2, 2)) * 2 + core


def dz_part(e_ref, s, t, hb_ref, dz):
    dim, blk = dz.shape
    rows = 32
    es = [[e_ref[s, N_TASK * c + t:N_TASK * c + t + 1, 128 * j:128 * j + 128] for j in range(blk // 128)]
          for c in range(N_CLASS)]
    for r0 in range(0, dim, rows):
        h = [hb_ref[N_CLASS * t + c, r0:r0 + rows, :] for c in range(N_CLASS)]
        for j in range(blk // 128):
            val = h[0] * es[0][j] + h[1] * es[1][j] + h[2] * es[2][j]
            dz[r0:r0 + rows, 128 * j:128 * j + 128] = val.astype(BF16)


def act_cols(x_ref, s, w1t_ref, ut, sl, lo, hi):
    act, slope = gelu_both(nt_dot(w1t_ref[...], x_ref[s, lo:hi, :]))
    ut[:, lo:hi] = act.astype(BF16)
    sl[:, lo:hi] = slope


def mega_kernel(n_total, x_hbm, w1_hbm, w2_hbm, heads_ref, lab_ref, wts_ref, out1_ref, out2_ref,
                x_all, e_all, w1v, w2v, w1f, w2f, w1t, w2s, hb, h24, part, act_far, g1, g2, rx1, rx2,
                dz0, dz1, da0, da1, ut0, ut1, sl0, sl1, gr_own, gr_all, tr_ref, rx_g1,
                ssem, rsem, lsem):
    m = lax.axis_index('model')
    d = lax.axis_index('data')
    core = lax.rem(d, 2)
    chip = d // 2
    me = m * N_DATA + d
    dim = x_all.shape[2]
    wide = w1v.shape[1]
    sl = w1t.shape[0]
    half = sl // 2
    p1 = dim // N_DATA
    p2 = wide // N_DATA

    lcopy = [pltpu.make_async_copy(x_hbm.at[pl.ds(pl.multiple_of((2 * m + k) * BLK, BLK), BLK), :], x_all.at[k], lsem.at[k])
             for k in range(2)]
    lcopy += [pltpu.make_async_copy(w1_hbm, w1v, lsem.at[2]), pltpu.make_async_copy(w2_hbm, w2v, lsem.at[3])]
    lcopy += [pltpu.make_async_copy(x_hbm.at[pl.ds(pl.multiple_of((2 - 2 * m + k) * BLK, BLK), BLK), :], x_all.at[2 + k],
                                    lsem.at[4 + k]) for k in range(2)]
    for cp in lcopy:
        cp.start()

    barrier = pltpu.get_barrier_semaphore()
    for k in range(1, N_DEV):
        p = lax.rem(me + k, N_DEV)
        pl.semaphore_signal(barrier, inc=1, device_id=(p // N_DATA, lax.rem(p, N_DATA)), device_id_type=MESH)
    pl.semaphore_wait(barrier, N_DEV - 1)

    twin = (1 - m, d)
    peer = (m, d + 1 - 2 * core)
    nb_x = (m, xor_data(d, 1))
    nb_y = (m, xor_data(d, 2))

    table = {}

    def rcopy(name, src, dst, dev):
        if name not in table:
            table[name] = len(table)
        k = table[name]
        return pltpu.make_async_remote_copy(src, dst, ssem.at[k], rsem.at[k], device_id=dev, device_id_type=MESH)

    def w1_rows(dr):
        return w1f.at[pl.ds(pl.multiple_of(xor_data(d, dr) * p1, p1), p1), :]

    def w2_rows(dr):
        return w2f.at[pl.ds(pl.multiple_of(xor_data(d, dr) * p2, p2), p2), :]

    rows_of = {1: w1_rows, 2: w2_rows}

    def w_copy(w, name, dr, dev):
        return rcopy(f'w{w}{name}', rows_of[w](dr), rows_of[w](dr), dev)

    wt = {1: rcopy('w1t', w1_hbm.at[pl.ds(pl.multiple_of(d * p1, p1), p1), :], w1_rows(0), twin),
          2: rcopy('w2t', w2_hbm.at[pl.ds(pl.multiple_of(d * p2, p2), p2), :], w2_rows(0), twin)}
    w_own = {(w, n): w_copy(w, 'own' + n, 0, dev) for w in (1, 2) for n, dev in (('p', peer), ('x', nb_x), ('y', nb_y))}
    w_peer = {(w, dr): w_copy(w, f'peer{dr}', dr, peer) for w in (1, 2) for dr in (1, 2, 3)}
    w_fwd = {1: w_copy(1, 'fwd', 1, nb_y), 2: w_copy(2, 'fwd', 2, nb_x)}

    def own_block(b, lo, n):
        return x_hbm.at[pl.ds(pl.multiple_of(b * BLK + lo, BLK // 2), n), :]

    hb2 = BLK // 2
    first_x = [rcopy(f'fx{h}', own_block(3 * m, h * hb2, hb2), x_all.at[4, pl.ds(h * hb2, hb2), :], nb_x) for h in (0, 1)]
    first_y = [rcopy(f'fy{h}', own_block(1 + m, h * hb2, hb2), x_all.at[5, pl.ds(h * hb2, hb2), :], nb_y) for h in (0, 1)]
    more_x = [rcopy(f'mx{b}', own_block(b, 0, BLK), x_all.at[s], nb_x) for b, s in ((1, 10), (2, 13))]
    more_y = [rcopy(f'my{b}', own_block(b, 0, BLK), x_all.at[s], nb_y) for b, s in ((0, 11), (3, 14))]
    fwd_x = rcopy('dx', x_all.at[5], x_all.at[8], nb_x)
    fwd_y = rcopy('dy', x_all.at[4], x_all.at[9], nb_y)
    z_x = [rcopy(f'zx{h}', x_all.at[4, pl.ds(h * hb2, hb2), :], x_all.at[6, pl.ds(h * hb2, hb2), :], twin) for h in (0, 1)]
    z_y = [rcopy(f'zy{h}', x_all.at[5, pl.ds(h * hb2, hb2), :], x_all.at[7, pl.ds(h * hb2, hb2), :], twin) for h in (0, 1)]
    z_d = [rcopy('zd8', x_all.at[8], x_all.at[12], twin), rcopy('zd9', x_all.at[9], x_all.at[15], twin)]

    k_out, k_in = m, 1 - m
    e_twin = [rcopy(f'et{k}', e_all.at[k], e_all.at[2 + k], twin) for k in range(2)]
    e_rest = []
    for dz in (0, 1):
        for dr in (1, 2, 3):
            dev = (lax.rem(m + dz, 2), xor_data(d, dr))
            s_out, s_in = {1: (4 + 2 * dz, 10 + 3 * m), 2: (11 + 3 * m, 5 + 2 * dz), 3: (9 + 6 * dz, 8 + 4 * dz)}[dr]
            e_rest.append(rcopy(f'eo{dz}{dr}', e_all.at[k_out], e_all.at[s_out], dev))
            e_rest.append(rcopy(f'ei{dz}{dr}', e_all.at[k_in], e_all.at[s_in], dev))

    wt[1].start()
    first_x[0].start()
    first_y[0].start()
    wt[2].start()

    h24[...] = jnp.zeros_like(h24)
    for t in range(N_TASK):
        h = heads_ref[t].astype(F32)
        for c in range(N_CLASS):
            hb[N_CLASS * t + c] = jnp.broadcast_to(h[:, c:c + 1], (dim, 128))
        ht = h.T
        for c in range(N_CLASS):
            h24[8 * c + t:8 * c + t + 1, :] = ht[c:c + 1, :]
    for k in range(4):
        lcopy[k].wait()
    off = pl.multiple_of(chip * sl, sl)
    w1t[...] = w1v[:, pl.ds(off, sl)].T
    w2s[...] = w2v[pl.ds(off, sl), :]

    fc = wide // 3

    def part_block(k):
        x = x_all[k]
        acc = None
        for f in range(0, wide, fc):
            u = gelu_only(nn_dot(x, w1v[:, f:f + fc])).astype(BF16)
            y = nn_dot(u, w2v[f:f + fc, :])
            acc = y if acc is None else acc + y
        part[k] = acc

    part_block(0)
    wt[1].wait_recv()
    for n in 'pxy':
        w_own[1, n].start()
    part_block(1)
    wt[2].wait_recv()
    for n in 'pxy':
        w_own[2, n].start()
    first_x[0].wait_recv()
    z_x[0].start()
    first_y[0].wait_recv()
    z_y[0].start()
    w_own[1, 'x'].wait_recv()
    w_fwd[1].start()
    w_peer[1, 1].start()
    w_own[1, 'y'].wait_recv()
    w_peer[1, 2].start()
    first_y[1].start()
    w_own[2, 'y'].wait_recv()
    w_fwd[2].start()
    w_peer[2, 2].start()
    first_x[1].start()
    w_own[2, 'x'].wait_recv()
    w_peer[2, 1].start()
    w_fwd[1].wait_recv()
    w_peer[1, 3].start()
    w_own[1, 'p'].wait_recv()
    for dr in (1, 2, 3):
        w_peer[1, dr].wait_recv()
    for k in range(2):
        x = x_all[k]
        for f in range(0, wide, fc):
            act_far[k, :, f:f + fc] = gelu_only(nn_dot(x, w1f[:, f:f + fc])).astype(BF16)
    w_fwd[2].wait_recv()
    w_peer[2, 3].start()
    w_own[2, 'p'].wait_recv()
    for dr in (1, 2, 3):
        w_peer[2, dr].wait_recv()
    heads24 = h24[...].astype(BF16)
    for k in range(2):
        mlp = part[k] + nn_dot(act_far[k], w2f[...])
        z = (x_all[k].astype(F32) + mlp).astype(BF16)
        logits = nt_dot(heads24, z)
        lg = [logits[8 * c:8 * c + N_TASK, :] for c in range(N_CLASS)]
        top = jnp.maximum(jnp.maximum(lg[0], lg[1]), lg[2])
        ex = [jnp.exp(v - top) for v in lg]
        tot = ex[0] + ex[1] + ex[2]
        lab = lab_ref[:, pl.ds(pl.multiple_of((2 * m + k) * BLK, BLK), BLK)]
        for c in range(N_CLASS):
            hot = jnp.where(lab == c, 1.0, 0.0)
            e_all[k, N_TASK * c:N_TASK * c + N_TASK, :] = (ex[c] / tot - hot) * (1.0 / n_total)
        e_all[k, 12:16, :] = jnp.zeros((4, BLK), F32)
    for cp in e_twin + e_rest:
        cp.start()

    dzs, das, uts, sls = (dz0, dz1), (da0, da1), (ut0, ut1), (sl0, sl1)
    n_blk = x_all.shape[0]
    g1[...] = jnp.zeros_like(g1)
    g2[...] = jnp.zeros_like(g2)
    for lo in range(0, BLK, 256):
        act_cols(x_all, 0, w1t, ut0, sl0, lo, lo + 256)
    dz_part(e_all, 0, 0, hb, dz0)

    def links_1():
        first_x[1].wait_recv()
        first_y[1].wait_recv()
        for cp in (fwd_x, fwd_y, z_x[1], z_y[1], more_x[0], more_y[0], more_x[1], more_y[1]):
            cp.start()

    def links_2():
        for cp in (fwd_x, fwd_y):
            cp.wait_recv()
        for cp in z_d:
            cp.start()

    def arrive(*cps):
        def go():
            for cp in cps:
                cp.wait_recv()
        return go

    actions = {1: [arrive(*e_twin)], 2: [links_1],
               3: [arrive(*e_rest)], 5: [arrive(*z_x)], 6: [arrive(*z_y), links_2],
               9: [arrive(more_x[0])], 10: [arrive(more_y[0])], 11: [arrive(z_d[0])], 12: [arrive(more_x[1])],
               13: [arrive(more_y[1])], 14: [arrive(z_d[1])]}
    lcopy[4].wait()
    lcopy[5].wait()

    def step(p, q):
        s = 2 * p + q
        for k, acts in actions.items():
            if k % 2 == q:
                @pl.when(p == k // 2)
                def _():
                    for act in acts:
                        act()
        nxt = jnp.minimum(s + 1, n_blk - 1)
        ut, slp = uts[q], sls[q]
        for t in range(N_TASK):
            dz, da = dzs[t % 2], das[t % 2]
            sn, tn = (s, t + 1) if t < N_TASK - 1 else (nxt, 0)
            rows = slice(t * sl, (t + 1) * sl)
            da[...] = (nn_dot(w2s[...], dz[...]) * slp[...]).astype(BF16)
            dz_part(e_all, sn, tn, hb, dzs[(t + 1) % 2])
            if t < 2:
                act_cols(x_all, nxt, w1t, uts[1 - q], sls[1 - q], 256 * t, 256 * t + 256)
            g2[rows, :] += nt_dot(ut[...], dz[...])
            g1[rows, :] += nn_dot(da[...], x_all[s])

    def pair(p, c):
        step(p, 0)
        step(p, 1)
        return c

    lax.fori_loop(0, n_blk // 2, pair, 0)

    keep = pl.multiple_of(core * half, half)
    give = pl.multiple_of((1 - core) * half, half)
    halves = [[rcopy(f'h{a}{t}', src.at[pl.ds(t * sl + give, half), :], dst.at[t], peer) for t in range(N_TASK)]
              for a, (src, dst) in enumerate(((g1, rx1), (g2, rx2)))]
    for cp in halves[0] + halves[1]:
        cp.start()
    pairs = [(i, j) for i in range(N_TASK) for j in range(i, N_TASK)]
    acc = tuple(jnp.zeros((8, 128), F32) for _ in pairs)
    for a, (src, dst) in enumerate(((g1, rx1), (g2, rx2))):
        for cp in halves[a]:
            cp.wait_recv()

        def fold(r, acc):
            row = pl.multiple_of(r * 8, 8)
            acc = list(acc)
            for l in range(0, dim, 128):
                gs = []
                for t in range(N_TASK):
                    v = dst[t, pl.ds(row, 8), l:l + 128] + src[pl.ds(pl.multiple_of(t * sl + keep + row, 8), 8), l:l + 128]
                    dst[t, pl.ds(row, 8), l:l + 128] = v
                    gs.append(v)
                for q, (i, j) in enumerate(pairs):
                    acc[q] = acc[q] + gs[i] * gs[j]
            return tuple(acc)

        acc = lax.fori_loop(0, half // 8, fold, acc)
    gr_own[...] = jnp.zeros_like(gr_own)
    for q in range(len(pairs)):
        gr_own[q:q + 1, :] = jnp.sum(acc[q], axis=0, keepdims=True)
    loc = pltpu.make_async_copy(gr_own, gr_all.at[me], lsem.at[6])
    loc.start()
    grams = []
    for k in range(1, N_DEV):
        p = lax.rem(me + k, N_DEV)
        grams.append(rcopy(f'gram{k}', gr_own, gr_all.at[me], (p // N_DATA, lax.rem(p, N_DATA))))
        grams[-1].start()

    w_sends = list(wt.values()) + list(w_own.values()) + list(w_peer.values()) + list(w_fwd.values())
    for cp in (w_sends + first_x + first_y + more_x + more_y + [fwd_x, fwd_y] + z_x + z_y + z_d + e_twin + e_rest
               + halves[0] + halves[1]):
        cp.wait_send()

    for cp in grams:
        cp.wait()
    loc.wait()
    tot = gr_all[0]
    for k in range(1, N_DEV):
        tot = tot + gr_all[k]
    sums = jnp.broadcast_to(jnp.sum(tot, axis=1, keepdims=True), tot.shape)
    gram = {}
    for q, (i, j) in enumerate(pairs):
        gram[i, j] = gram[j, i] = sums[q:q + 1, :]
    scale = (gram[0, 0] + gram[1, 1] + gram[2, 2] + gram[3, 3]) / N_TASK

    def eg_step(k, w):
        up = []
        for i in range(N_TASK):
            mv = (gram[i, 0] * w[0] + gram[i, 1] * w[1]) + (gram[i, 2] * w[2] + gram[i, 3] * w[3])
            up.append(w[i] * jnp.exp(-mv / scale))
        s = (up[0] + up[1]) + (up[2] + up[3])
        return tuple(u / s for u in up)

    w = lax.fori_loop(0, STEPS, eg_step, tuple(jnp.full((1, 128), 1.0 / N_TASK, F32) for _ in range(N_TASK)))
    wts_ref[...] = jnp.zeros_like(wts_ref)
    for t in range(N_TASK):
        wts_ref[t:t + 1, :] = w[t]
    wb = [jnp.broadcast_to(v, (half, 128)) for v in w]

    def blend(rx, l):
        v = wb[0] * rx[0, :, l:l + 128]
        for t in range(1, N_TASK):
            v = v + wb[t] * rx[t, :, l:l + 128]
        return v

    for l in range(0, dim, 128):
        tr_ref[l:l + 128, 0:half] = blend(rx1, l).T
    outs = []
    for k in range(1, N_DATA):
        p = lax.rem(d + k, N_DATA)
        outs.append(rcopy(f'out{k}', tr_ref.at[pl.ds(pl.multiple_of(p * p1, p1), p1), :], rx_g1.at[d], (m, p)))
        outs[-1].start()
    loc = pltpu.make_async_copy(tr_ref.at[pl.ds(pl.multiple_of(d * p1, p1), p1), :], rx_g1.at[d], lsem.at[7])
    loc.start()
    for l in range(0, dim, 128):
        out2_ref[:, l:l + 128] = blend(rx2, l)
    loc.wait()
    for cp in outs:
        cp.wait()
    for k in range(N_DATA):
        out1_ref[:, k * half:(k + 1) * half] = rx_g1[k, :, 0:half]
    assert len(table) <= ssem.shape[0]


def mega_call(n_total, tokens, w_up, w_down, task_heads, labels):
    n_loc, dim = tokens.shape
    wide = w_up.shape[1]
    sl = 2 * wide // N_DATA
    half = sl // 2
    per = dim // N_DATA
    n_half = n_loc // 2
    vm = pl.BlockSpec(memory_space=pltpu.VMEM)
    hbm = pl.BlockSpec(memory_space=pl.ANY)
    vmem = pltpu.VMEM
    return pl.pallas_call(
        functools.partial(mega_kernel, n_total),
        out_shape=[jax.ShapeDtypeStruct((8, 128), F32), jax.ShapeDtypeStruct((per, half * N_DATA), F32),
                   jax.ShapeDtypeStruct((half, dim), F32)],
        in_specs=[hbm, hbm, hbm, vm, vm],
        out_specs=[vm, vm, vm],
        scratch_shapes=[vmem((4 * n_loc // BLK, BLK, dim), BF16), vmem((4 * n_loc // BLK, 16, BLK), F32),
                        vmem((dim, wide), BF16), vmem((wide, dim), BF16), vmem((dim, wide), BF16), vmem((wide, dim), BF16),
                        vmem((sl, dim), BF16), vmem((sl, dim), BF16),
                        vmem((N_TASK * N_CLASS, dim, 128), F32), vmem((24, dim), F32),
                        vmem((2, n_half // 2, dim), F32), vmem((2, n_half // 2, wide), BF16),
                        vmem((N_TASK * sl, dim), F32), vmem((N_TASK * sl, dim), F32),
                        vmem((N_TASK, half, dim), F32), vmem((N_TASK, half, dim), F32),
                        vmem((dim, BLK), BF16), vmem((dim, BLK), BF16), vmem((sl, BLK), BF16), vmem((sl, BLK), BF16),
                        vmem((sl, BLK), BF16), vmem((sl, BLK), BF16), vmem((sl, BLK), F32), vmem((sl, BLK), F32),
                        vmem((16, 128), F32), vmem((N_DEV, 16, 128), F32), vmem((dim, 256), F32), vmem((N_DATA, per, 256), F32),
                        pltpu.SemaphoreType.DMA((88,)), pltpu.SemaphoreType.DMA((88,)), pltpu.SemaphoreType.DMA((8,))],
        compiler_params=pltpu.CompilerParams(vmem_limit_bytes=VMEM_LIMIT, collective_id=0, has_side_effects=True),
    )(tokens, w_up, w_down, task_heads, labels)


def solution(mesh):
    n_data = mesh.shape['data']

    def local_step(tokens, w_up, w_down, task_heads, labels):
        wts, grad_up, grad_down = mega_call(tokens.shape[0] * n_data, tokens, w_up, w_down, task_heads, labels)
        return wts[:N_TASK, 0], grad_up, grad_down

    return jax.shard_map(
        local_step, mesh=mesh,
        in_specs=(P('data', None), P(None, 'model'), P('model', None), P(None, None, None), P(None, 'data')),
        out_specs=(P(None), P('data', 'model'), P(('model', 'data'), None)),
        check_vma=False)
```

time: 886 us -> 161 us (0.18)
  waiting for transfers between devices: 572 us -> 0 us
  matrix products: 159 us -> 0 us
  Pallas kernels: 0 us -> 153 us
  local copies, waits for them, and re-layouts: 69.2 us -> 7.08 us
  blocking collectives: 30.9 us -> 0 us
  other arithmetic: 28.4 us -> 0 us
  between operations: 16.6 us -> 0.64 us
    unnamed x3 -> x0, waiting for transfers between devices: 435 us -> none
    dot_general x11 -> x0, matrix products: 159 us -> none  [the longest x1 29.1 us: local_step(): jnp.einsum('tbd,fd->tbf', d_trunk, w_down, preferred_element_type=jnp.flo...]
    pallas_call x0 -> x1, Pallas kernels: none -> 153 us  [mega_call(): pl.pallas_call(functools.partial(mega_kernel, n_total), out_shape=[jax.Sh...]
    psum x1 -> x0, waiting for transfers between devices: 138 us -> none  [local_step(): mlp_out = lax.psum(part_out, 'model')]
    transpose x2 -> x0, local copies, waits for them, and re-layouts: 44.7 us -> none  [the longest x1 22.8 us: local_step(): jnp.einsum('bd,tbf->tdf', tokens, d_pre, preferred_element_type=jnp.float32)]
    psum x1 -> x0, blocking collectives: 30.9 us -> none  [local_step(): gram_mat = lax.psum(gram_part, ('model', 'data'))]
    reduce_sum x42 -> x0, other arithmetic: 15.3 us -> none  [the longest x20 12.4 us: eg_step(): return updated / jnp.sum(updated)]
    div x21 -> x0, other arithmetic: 13 us -> none  [the longest x20 13 us: eg_step(): return updated / jnp.sum(updated)]
  transfers between devices with their start and end apart: 2 -> 0, of which waited for: 2 -> 0; matrix products, arithmetic and copies ran while one was open for 2% -> 0% of each run, Pallas kernels for 0% -> 0%
where the time goes in v2:
time: 161 us
  Pallas kernels  153 us (95%)
  local copies, waits for them, and re-layouts  7.08 us (4%)
    pallas_call x1, Pallas kernels, mega_call(): pl.pallas_call(functools.partial(mega_kernel, n_total), out_shape=[jax.Sh...  153 us
    unnamed x3, local copies, waits for them, and re-layouts  5.77 us

profile of v2, /device:TPU:1, one launch (start us, length us, event | category | flops | bytes accessed | tf_op | source)
XLA Modules:
  0.0 160.9 jit_solution(3810787153955043780)
XLA Ops:
  0.6 1.9 %copy.9.heads_ref = bf16[4,768,3]{2,1,0:T(8,128)(2,1)} copy(bf16[4,768,3]{1,0,2:T(4,128)(2,1)} %param.8) | data formatting | bytes 36864 | tf_op args[3]
  2.6 153.2 %shard_map.76 = (f32[8,128]{1,0:T(8,128)}, f32[96,1536]{1,0:T(8,128)}, f32[192,768]{1,0:T(8,128)}) custom-call(bf16[2048,768]{1,0:T(8,128)(2,1)} %x_hbm.1, bf16[768,1536]{1,0:T(8,128)(2,1)} %w1_hbm.1, bf16[1536,768]{1,0:T(8,128)(2,1)} %w2_hbm.1, bf16[4,768,3]{2,1,0:T(8,128)(2,1)} %copy.9.heads_ref, s32[4,2048]{1,0:T(4,128)} %lab_ref.1), custom_call_target="tpu_custom_call" | custom-call | tf_op jit(solution)/shard_map/pallas_call | solution.py:402
  155.8 1.3 slice_reduce_fusion
  157.1 1.9 %copy.12 = f32[96,1536]{1,0:T(8,128)} copy(f32[96,1536]{1,0:T(8,128)} %get-tuple-element.13) | data formatting | bytes 1179648
  159.0 1.9 %copy.13 = f32[192,768]{1,0:T(8,128)} copy(f32[192,768]{1,0:T(8,128)} %get-tuple-element.14) | data formatting | bytes 1179648

commit v3 on v0

v3 whole, which is shorter than its diff:
```python
import functools

import jax
import jax.numpy as jnp
from jax import lax
from jax.experimental import pallas as pl
from jax.experimental.pallas import tpu as pltpu
from jax.sharding import PartitionSpec as P

STEPS = 20
MESH = pl.DeviceIdType.MESH
F32 = jnp.float32
BF16 = jnp.bfloat16
C0 = 0.7978845608028654
C1 = 0.044715
N_DATA = 8
N_DEV = 16
N_TASK = 4
N_CLASS = 3
BLK = 512
VMEM_LIMIT = 63 * 1024 * 1024


def gelu_only(a):
    return a * (0.5 + 0.5 * jnp.tanh(a * (C0 + (C0 * C1) * (a * a))))


def gelu_both(a):
    a2 = a * a
    t = jnp.tanh(a * (C0 + (C0 * C1) * a2))
    h = 0.5 + 0.5 * t
    slope = h + (0.5 * a) * (1.0 - t * t) * (C0 + (3.0 * C0 * C1) * a2)
    return a * h, slope


def nt_dot(a, b):
    return lax.dot_general(a, b, (((1,), (1,)), ((), ())), preferred_element_type=F32)


def nn_dot(a, b):
    return jnp.dot(a, b, preferred_element_type=F32)


def xor_data(d, dr):
    core = lax.rem(d, 2)
    x = lax.rem(d // 2, 2)
    y = d // 4
    return (lax.rem(y + dr // 2, 2) * 2 + lax.rem(x + dr % 2, 2)) * 2 + core


def dz_part(e_ref, s, t, hb_ref, dz):
    dim, blk = dz.shape
    rows = 32
    es = [[e_ref[s, N_TASK * c + t:N_TASK * c + t + 1, lo:lo + 128] for lo in range(0, blk, 128)] for c in range(N_CLASS - 1)]
    for r0 in range(0, dim, rows):
        h = [hb_ref[(N_CLASS - 1) * t + c, r0:r0 + rows, :] for c in range(N_CLASS - 1)]
        for j in range(blk // 128):
            val = h[0] * es[0][j] + h[1] * es[1][j]
            dz[r0:r0 + rows, 128 * j:128 * j + 128] = val.astype(BF16)


def act_part(x, w1t_ref, ut, sl, lo):
    act, slope = gelu_both(nt_dot(w1t_ref[...], x))
    ut[:, lo:lo + x.shape[0]] = act.astype(BF16)
    sl[:, lo:lo + x.shape[0]] = slope


def mega_kernel(n_total, x_hbm, w1_hbm, w2_hbm, heads_ref, lab_ref, wts_ref, out1_ref, out2_ref,
                x_all, e_all, w1v, w2v, w1f, w2f, w1t, w2s, hb, part, act_far, g1, g2, rx1, rx2,
                dz00, dz01, dz10, dz11, da00, da01, da10, da11, ut0, ut1, ut2, sl0, sl1, sl2, gr_own, gr_all, tr_ref, rx_g1,
                ssem, rsem, lsem, osend, orecv):
    m = lax.axis_index('model')
    d = lax.axis_index('data')
    core = lax.rem(d, 2)
    chip = d // 2
    me = m * N_DATA + d
    dim = x_all.shape[1]
    wide = w1v.shape[1]
    sl = w1t.shape[0]
    half = sl // 2
    p1 = dim // N_DATA
    p2 = wide // N_DATA

    def slot(k, lo=0, n=BLK):
        return x_all.at[pl.ds(k * BLK + lo, n), :]

    lcopy = [pltpu.make_async_copy(x_hbm.at[pl.ds(pl.multiple_of((2 * m + k) * BLK, BLK), BLK), :], slot(k), lsem.at[k])
             for k in range(2)]
    lcopy += [pltpu.make_async_copy(w1_hbm, w1v, lsem.at[2]), pltpu.make_async_copy(w2_hbm, w2v, lsem.at[3])]
    lcopy += [pltpu.make_async_copy(x_hbm.at[pl.ds(pl.multiple_of((2 - 2 * m + k) * BLK, BLK), BLK), :], slot(2 + k),
                                    lsem.at[4 + k]) for k in range(2)]
    for cp in lcopy:
        cp.start()

    barrier = pltpu.get_barrier_semaphore()
    for k in range(1, N_DEV):
        p = lax.rem(me + k, N_DEV)
        pl.semaphore_signal(barrier, inc=1, device_id=(p // N_DATA, lax.rem(p, N_DATA)), device_id_type=MESH)
    pl.semaphore_wait(barrier, N_DEV - 1)

    twin = (1 - m, d)
    peer = (m, d + 1 - 2 * core)
    nb_x = (m, xor_data(d, 1))
    nb_y = (m, xor_data(d, 2))

    table = {}

    def rcopy(name, src, dst, dev):
        if name not in table:
            table[name] = len(table)
        k = table[name]
        return pltpu.make_async_remote_copy(src, dst, ssem.at[k], rsem.at[k], device_id=dev, device_id_type=MESH)

    def w1_rows(dr):
        return w1f.at[pl.ds(pl.multiple_of(xor_data(d, dr) * p1, p1), p1), :]

    def w2_rows(dr):
        return w2f.at[pl.ds(pl.multiple_of(xor_data(d, dr) * p2, p2), p2), :]

    rows_of = {1: w1_rows, 2: w2_rows}

    def w_copy(w, name, dr, dev):
        return rcopy(f'w{w}{name}', rows_of[w](dr), rows_of[w](dr), dev)

    wt = {1: rcopy('w1t', w1_hbm.at[pl.ds(pl.multiple_of(d * p1, p1), p1), :], w1_rows(0), twin),
          2: rcopy('w2t', w2_hbm.at[pl.ds(pl.multiple_of(d * p2, p2), p2), :], w2_rows(0), twin)}
    w_own = {(w, n): w_copy(w, 'own' + n, 0, dev) for w in (1, 2) for n, dev in (('p', peer), ('x', nb_x), ('y', nb_y))}
    w_peer = {(w, dr): w_copy(w, f'peer{dr}', dr, peer) for w in (1, 2) for dr in (1, 2, 3)}
    w_diag = {1: rcopy('w1d', w1_hbm.at[pl.ds(pl.multiple_of(xor_data(d, 3) * p1, p1), p1), :], w1_rows(3), twin),
              2: rcopy('w2d', w2_hbm.at[pl.ds(pl.multiple_of(xor_data(d, 3) * p2, p2), p2), :], w2_rows(3), twin)}

    def own_block(b, lo, n):
        return x_hbm.at[pl.ds(pl.multiple_of(b * BLK + lo, BLK // 2), n), :]

    hb2 = BLK // 2
    first_x = [rcopy(f'fx{h}', own_block(3 * m, h * hb2, hb2), slot(4, h * hb2, hb2), nb_x) for h in (0, 1)]
    first_y = [rcopy(f'fy{h}', own_block(1 + m, h * hb2, hb2), slot(5, h * hb2, hb2), nb_y) for h in (0, 1)]
    more_x = [rcopy(f'mx{b}', own_block(b, 0, BLK), slot(k), nb_x) for b, k in ((1, 10), (2, 13))]
    more_y = [rcopy(f'my{b}', own_block(b, 0, BLK), slot(k), nb_y) for b, k in ((0, 11), (3, 14))]
    fwd_x = [rcopy(f'dx{h}', slot(5, h * hb2, hb2), slot(6, h * hb2, hb2), nb_x) for h in (0, 1)]
    fwd_y = [rcopy(f'dy{h}', slot(4, h * hb2, hb2), slot(7, h * hb2, hb2), nb_y) for h in (0, 1)]
    z_x = [rcopy(f'zx{h}', slot(4, h * hb2, hb2), slot(8, h * hb2, hb2), twin) for h in (0, 1)]
    z_y = [rcopy(f'zy{h}', slot(5, h * hb2, hb2), slot(9, h * hb2, hb2), twin) for h in (0, 1)]
    z_d = [rcopy('zd6', slot(6), slot(12), twin), rcopy('zd7', slot(7), slot(15), twin)]

    k_out, k_in = m, 1 - m
    e_twin = [rcopy(f'et{k}', e_all.at[k], e_all.at[2 + k], twin) for k in range(2)]
    e_rest = []
    for dz in (0, 1):
        for dr in (1, 2, 3):
            dev = (lax.rem(m + dz, 2), xor_data(d, dr))
            s_out, s_in = {1: (4 + 4 * dz, 10 + 3 * m), 2: (11 + 3 * m, 5 + 4 * dz), 3: (7 + 8 * dz, 6 + 6 * dz)}[dr]
            e_rest.append(rcopy(f'eo{dz}{dr}', e_all.at[k_out], e_all.at[s_out], dev))
            e_rest.append(rcopy(f'ei{dz}{dr}', e_all.at[k_in], e_all.at[s_in], dev))

    wt[1].start()
    first_x[0].start()
    first_y[0].start()
    wt[2].start()
    w_diag[1].start()
    w_diag[2].start()

    for c in range(N_CLASS - 1):
        h = heads_ref[c].astype(F32) - heads_ref[N_CLASS - 1].astype(F32)
        h = jnp.concatenate([h, h], axis=0).T
        for t in range(N_TASK):
            hb[(N_CLASS - 1) * t + c] = jnp.broadcast_to(h[:, t:t + 1], (dim, 128))
    for k in range(4):
        lcopy[k].wait()
    off = pl.multiple_of(chip * sl, sl)
    w1t[...] = w1v[:, pl.ds(off, sl)].T
    w2s[...] = w2v[pl.ds(off, sl), :]

    fc = wide // 3

    def part_block(k):
        x = x_all[k * BLK:(k + 1) * BLK, :]
        acc = None
        for f in range(0, wide, fc):
            u = gelu_only(nn_dot(x, w1v[:, f:f + fc])).astype(BF16)
            y = nn_dot(u, w2v[f:f + fc, :])
            acc = y if acc is None else acc + y
        part[k] = acc

    with jax.named_scope('near'):
        part_block(0)
        wt[1].wait_recv()
        for n in 'xyp':
            w_own[1, n].start()
        part_block(1)
        wt[2].wait_recv()
        for n in 'xyp':
            w_own[2, n].start()
        first_x[1].start()
        first_y[1].start()
        first_x[0].wait_recv()
        z_x[0].start()
        first_y[0].wait_recv()
        fwd_x[0].start()
        fwd_y[0].start()
        act_part(x_all[0:BLK, :], w1t, ut0, sl0, 0)
        g1[...] = jnp.zeros_like(g1)
        g2[...] = jnp.zeros_like(g2)
    with jax.named_scope('wait_w1'):
        w_own[1, 'x'].wait_recv()
        w_peer[1, 1].start()
        w_own[1, 'y'].wait_recv()
        w_peer[1, 2].start()
        w_diag[1].wait_recv()
        w_peer[1, 3].start()
        w_own[1, 'p'].wait_recv()
        for dr in (1, 2, 3):
            w_peer[1, dr].wait_recv()
    with jax.named_scope('far1'):
        for k in range(2):
            x = x_all[k * BLK:(k + 1) * BLK, :]
            for f in range(0, wide, fc):
                act_far[k, :, f:f + fc] = gelu_only(nn_dot(x, w1f[:, f:f + fc])).astype(BF16)
    def w2_chunk(k, dr):
        rows = pl.ds(pl.multiple_of((xor_data(d, dr) // 2) * sl, sl), sl)
        part[k] += nn_dot(act_far[k, :, rows], w2f[rows, :])

    with jax.named_scope('wait_w2'):
        w_own[2, 'x'].wait_recv()
        w_peer[2, 1].start()
        w_own[2, 'y'].wait_recv()
        w_peer[2, 2].start()
        w_own[2, 'p'].wait_recv()
        for k in range(2):
            w2_chunk(k, 0)
        for dr in (1, 2):
            w_peer[2, dr].wait_recv()
            for k in range(2):
                w2_chunk(k, dr)
        w_diag[2].wait_recv()
        w_peer[2, 3].start()
        w_peer[2, 3].wait_recv()
    with jax.named_scope('errs'):
        heads16 = jnp.concatenate([heads_ref[c] for c in range(N_CLASS)] + [heads_ref[0]], axis=0)
        for k in range(2):
            w2_chunk(k, 3)
            z = (x_all[k * BLK:(k + 1) * BLK, :].astype(F32) + part[k]).astype(BF16)
            logits = nt_dot(heads16, z)
            lg = [logits[N_TASK * c:N_TASK * c + N_TASK, :] for c in range(N_CLASS)]
            top = jnp.maximum(jnp.maximum(lg[0], lg[1]), lg[2])
            ex = [jnp.exp(v - top) for v in lg]
            tot = ex[0] + ex[1] + ex[2]
            lab = lab_ref[:, pl.ds(pl.multiple_of((2 * m + k) * BLK, BLK), BLK)]
            for c in range(N_CLASS - 1):
                rest = (ex[1 - c] + ex[2]) / tot
                e_all[k, N_TASK * c:N_TASK * c + N_TASK, :] = jnp.where(lab == c, -rest, ex[c] / tot) * (1.0 / n_total)
        for cp in e_twin + e_rest:
            cp.start()
        z_y[0].start()

    dzs, das, uts, sls = ((dz00, dz01), (dz10, dz11)), ((da00, da01), (da10, da11)), (ut0, ut1, ut2), (sl0, sl1, sl2)
    n_blk = x_all.shape[0] // BLK
    keep_row = pl.multiple_of(core * half, half)
    give_row = pl.multiple_of((1 - core) * half, half)
    keep_col = pl.multiple_of(core * (dim // 2), 128)
    give_col = pl.multiple_of((1 - core) * (dim // 2), 128)
    halves = [(rcopy(f'h1{t}', g1.at[pl.ds(t * sl, sl), pl.ds(give_col, dim // 2)], rx1.at[t], peer),
               rcopy(f'h2{t}', g2.at[pl.ds(t * sl + give_row, half), :], rx2.at[t], peer)) for t in range(N_TASK)]

    with jax.named_scope('lead_in'):
        dz_part(e_all, 0, 0, hb, dz00)
        first_x[1].wait_recv()
        first_y[1].wait_recv()
        for cp in (fwd_x[1], fwd_y[1], z_x[1], z_y[1], more_x[0], more_y[0], more_x[1], more_y[1]):
            cp.start()

    def links_2():
        for cp in fwd_x + fwd_y:
            cp.wait_recv()
        for cp in z_d:
            cp.start()

    def arrive(*cps):
        def go():
            for cp in cps:
                cp.wait_recv()
        return go

    lcopy[4].wait()
    lcopy[5].wait()
    actions = {1: arrive(*e_twin), 3: arrive(*e_rest), 5: links_2, 7: arrive(*z_x), 8: arrive(*z_y), 9: arrive(more_x[0]),
               10: arrive(more_y[0]), 11: arrive(z_d[0]), 12: arrive(more_x[1]), 13: arrive(more_y[1])}

    def tok(b, lo=0, n=BLK):
        return pl.ds(pl.multiple_of(b * BLK + lo, 256), n)

    def total(parts):
        out = parts[0]
        for v in parts[1:]:
            out = out + v
        return out

    def group(blks, nxt, last):
        hw = BLK // 2
        for t in range(N_TASK):
            dz, da = dzs[t % 2], das[t % 2]
            rows = slice(t * sl, (t + 1) * sl)
            for b, u, h in blks:
                da[h][...] = (nn_dot(w2s[...], dz[h][...]) * sls[u][...]).astype(BF16)
            if t < N_TASK - 1:
                for b, u, h in blks:
                    dz_part(e_all, b, t + 1, hb, dzs[(t + 1) % 2][h])
            elif nxt is not None:
                dz_part(e_all, nxt[0], 0, hb, dzs[0][nxt[2]])
            if t < 2 and nxt is not None:
                act_part(x_all[tok(nxt[0], t * hw, hw), :], w1t, uts[nxt[1]], sls[nxt[1]], t * hw)
            g2[rows, :] += total([nt_dot(uts[u][...], dz[h][...]) for b, u, h in blks])
            g1[rows, :] += total([nn_dot(da[h][...], x_all[tok(b), :]) for b, u, h in blks])
            if last:
                for cp in halves[t]:
                    cp.start()

    def body(i, c):
        for q in (0, 1):
            for k, act in actions.items():
                if k % 2 == q:
                    @pl.when(i == k // 2)
                    def _():
                        with jax.named_scope(f'arr{k}'):
                            act()
            group([(2 * i + q, q, 0)], (2 * i + q + 1, 1 - q, 0), False)
        return c

    with jax.named_scope('main'):
        lax.fori_loop(0, n_blk // 2 - 1, body, 0)
    with jax.named_scope('last_act'):
        z_d[1].wait_recv()
        act_part(x_all[tok(n_blk - 1), :], w1t, ut2, sl2, 0)
        dz_part(e_all, n_blk - 1, 0, hb, dz01)
    with jax.named_scope('main_last'):
        group([(n_blk - 2, 0, 0), (n_blk - 1, 2, 1)], None, True)

    with jax.named_scope('halves'):
        pairs = [(i, j) for i in range(N_TASK) for j in range(i, N_TASK)]
        acc = tuple(jnp.zeros((8, 128), F32) for _ in pairs)

        def fold(new, old, acc):
            def one(src, dst, n_rows, n_cols, row_of, col0, acc):
                def go(r, acc):
                    row = pl.multiple_of(r * 8, 8)
                    acc = list(acc)
                    for l in range(0, n_cols, 128):
                        gs = {t: dst[t, pl.ds(row, 8), l:l + 128] for t in old}
                        for t in new:
                            v = dst[t, pl.ds(row, 8), l:l + 128] + src[pl.ds(pl.multiple_of(row_of(t) + row, 8), 8),
                                                                       pl.ds(pl.multiple_of(col0 + l, 128), 128)]
                            dst[t, pl.ds(row, 8), l:l + 128] = v
                            gs[t] = v
                        for q, (i, j) in enumerate(pairs):
                            if (i in new or j in new) and i in gs and j in gs:
                                acc[q] = acc[q] + gs[i] * gs[j]
                    return tuple(acc)
                return lax.fori_loop(0, n_rows // 8, go, acc)

            for t in new:
                for cp in halves[t]:
                    cp.wait_recv()
            acc = one(g1, rx1, sl, dim // 2, lambda t: t * sl, keep_col, acc)
            return one(g2, rx2, half, dim, lambda t: t * sl + keep_row, 0, acc)

        acc = fold((0, 1, 2), (), acc)
        acc = fold((3,), (0, 1, 2), acc)
    with jax.named_scope('gram_x'):
        gr_own[...] = jnp.zeros_like(gr_own)
        for q in range(len(pairs)):
            gr_own[q:q + 1, :] = jnp.sum(acc[q], axis=0, keepdims=True)
        loc = pltpu.make_async_copy(gr_own, gr_all.at[me], lsem.at[6])
        loc.start()
        grams = []
        for k in range(1, N_DEV):
            p = lax.rem(me + k, N_DEV)
            grams.append(rcopy(f'gram{k}', gr_own, gr_all.at[me], (p // N_DATA, lax.rem(p, N_DATA))))
            grams[-1].start()

        w_sends = list(wt.values()) + list(w_own.values()) + list(w_peer.values()) + list(w_diag.values())
        for cp in (w_sends + first_x + first_y + more_x + more_y + fwd_x + fwd_y + z_x + z_y + z_d + e_twin + e_rest
                   + [cp for h in halves for cp in h]):
            cp.wait_send()

        for cp in grams:
            cp.wait()
        loc.wait()
    with jax.named_scope('weights'):
        tot = gr_all[0]
        for k in range(1, N_DEV):
            tot = tot + gr_all[k]
        sums = jnp.broadcast_to(jnp.sum(tot, axis=1, keepdims=True), tot.shape)
        gram = {}
        for q, (i, j) in enumerate(pairs):
            gram[i, j] = gram[j, i] = sums[q:q + 1, :]
        scale = (gram[0, 0] + gram[1, 1] + gram[2, 2] + gram[3, 3]) / N_TASK

        def eg_step(k, w):
            up = []
            for i in range(N_TASK):
                mv = (gram[i, 0] * w[0] + gram[i, 1] * w[1]) + (gram[i, 2] * w[2] + gram[i, 3] * w[3])
                up.append(w[i] * jnp.exp(-mv / scale))
            s = (up[0] + up[1]) + (up[2] + up[3])
            return tuple(u / s for u in up)

        w = lax.fori_loop(0, STEPS, eg_step, tuple(jnp.full((1, 128), 1.0 / N_TASK, F32) for _ in range(N_TASK)))
        wts_ref[...] = jnp.zeros_like(wts_ref)
        for t in range(N_TASK):
            wts_ref[t:t + 1, :] = w[t]
    def blend(rx, l):
        wb = [jnp.broadcast_to(v, (rx.shape[1], 128)) for v in w]
        v = wb[0] * rx[0, :, l:l + 128]
        for t in range(1, N_TASK):
            v = v + wb[t] * rx[t, :, l:l + 128]
        return v

    with jax.named_scope('outs'):
        cols = pl.ds(pl.multiple_of(chip * sl, sl), sl)
        n_dest = N_DATA // 2
        outs = []
        for j in range(n_dest):
            p = n_dest * core + j
            src = tr_ref.at[j * p1:(j + 1) * p1, :]
            outs.append((p, pltpu.make_async_remote_copy(src, rx_g1.at[:, cols], osend.at[j], orecv.at[chip],
                                                         device_id=(m, p), device_id_type=MESH),
                         pltpu.make_async_copy(src, rx_g1.at[:, cols], lsem.at[7])))
        for l in range(0, dim // 2, 128):
            tr_ref[l:l + 128, :] = blend(rx1, l).T
        for p, far, near in outs:
            @pl.when(p != d)
            def _():
                far.start()

            @pl.when(p == d)
            def _():
                near.start()
        for l in range(0, dim, 128):
            out2_ref[:, l:l + 128] = blend(rx2, l)
        for k in range(N_DATA // 2):
            @pl.when(jnp.logical_or(core != d // n_dest, chip != k))
            def _():
                pltpu.make_async_remote_copy(tr_ref.at[0:p1, :], rx_g1.at[:, k * sl:(k + 1) * sl], osend.at[0], orecv.at[k],
                                             device_id=peer, device_id_type=MESH).wait_recv()
        for p, far, near in outs:
            @pl.when(p != d)
            def _():
                far.wait_send()

            @pl.when(p == d)
            def _():
                near.wait()
        out1_ref[...] = rx_g1[...]
    assert len(table) <= ssem.shape[0]


def mega_call(n_total, tokens, w_up, w_down, task_heads, labels):
    n_loc, dim = tokens.shape
    wide = w_up.shape[1]
    sl = 2 * wide // N_DATA
    half = sl // 2
    per = dim // N_DATA
    n_half = n_loc // 2
    vm = pl.BlockSpec(memory_space=pltpu.VMEM)
    hbm = pl.BlockSpec(memory_space=pl.ANY)
    vmem = pltpu.VMEM
    return pl.pallas_call(
        functools.partial(mega_kernel, n_total),
        out_shape=[jax.ShapeDtypeStruct((8, 128), F32), jax.ShapeDtypeStruct((per, half * N_DATA), F32),
                   jax.ShapeDtypeStruct((half, dim), F32)],
        in_specs=[hbm, hbm, hbm, vm, vm],
        out_specs=[vm, vm, vm],
        scratch_shapes=[vmem((4 * n_loc, dim), BF16), vmem((4 * n_loc // BLK, 8, BLK), F32),
                        vmem((dim, wide), BF16), vmem((wide, dim), BF16), vmem((dim, wide), BF16), vmem((wide, dim), BF16),
                        vmem((sl, dim), BF16), vmem((sl, dim), BF16),
                        vmem((N_TASK * (N_CLASS - 1), dim, 128), F32),
                        vmem((2, n_half // 2, dim), F32), vmem((2, n_half // 2, wide), BF16),
                        vmem((N_TASK * sl, dim), F32), vmem((N_TASK * sl, dim), F32),
                        vmem((N_TASK, sl, dim // 2), F32), vmem((N_TASK, half, dim), F32),
                        *[vmem((dim, BLK), BF16)] * 4, *[vmem((sl, BLK), BF16)] * 7, *[vmem((sl, BLK), F32)] * 3,
                        vmem((16, 128), F32), vmem((N_DEV, 16, 128), F32), vmem((dim // 2, sl), F32), vmem((per, wide), F32),
                        pltpu.SemaphoreType.DMA((88,)), pltpu.SemaphoreType.DMA((88,)), pltpu.SemaphoreType.DMA((8,)),
                        pltpu.SemaphoreType.DMA((4,)), pltpu.SemaphoreType.DMA((4,))],
        compiler_params=pltpu.CompilerParams(vmem_limit_bytes=VMEM_LIMIT, collective_id=0, has_side_effects=True),
    )(tokens, w_up, w_down, task_heads, labels)


def final_kernel(wts_in, g1_in, g2_in, wts_ref, g1_ref, g2_ref):
    for t in range(N_TASK):
        wts_ref[t] = wts_in[t, 0]
    g1_ref[...] = g1_in[...]
    g2_ref[...] = g2_in[...]


def final_call(wts, g1, g2):
    vm = pl.BlockSpec(memory_space=pltpu.VMEM)
    return pl.pallas_call(
        final_kernel,
        out_shape=[jax.ShapeDtypeStruct((N_TASK,), F32), jax.ShapeDtypeStruct(g1.shape, F32), jax.ShapeDtypeStruct(g2.shape, F32)],
        in_specs=[vm, vm, vm],
        out_specs=[pl.BlockSpec(memory_space=pltpu.SMEM), vm, vm],
        compiler_params=pltpu.CompilerParams(vmem_limit_bytes=VMEM_LIMIT),
    )(wts, g1, g2)


def solution(mesh):
    n_data = mesh.shape['data']

    def local_step(tokens, w_up, w_down, task_heads, labels):
        wts, up, down = mega_call(tokens.shape[0] * n_data, tokens, w_up, w_down, task_heads.transpose(2, 0, 1), labels)
        return final_call(wts, up, down)

    return jax.shard_map(
        local_step, mesh=mesh,
        in_specs=(P('data', None), P(None, 'model'), P('model', None), P(None, None, None), P(None, 'data')),
        out_specs=(P(None), P('data', 'model'), P(('model', 'data'), None)),
        check_vma=False)
```

time: 886 us -> 139 us (0.16)
  waiting for transfers between devices: 572 us -> 0 us
  matrix products: 159 us -> 0 us
  Pallas kernels: 0 us -> 138 us
  local copies, waits for them, and re-layouts: 69.2 us -> 0 us
  blocking collectives: 30.9 us -> 0 us
  other arithmetic: 28.4 us -> 0 us
  between operations: 16.6 us -> 0.82 us
    unnamed x3 -> x0, waiting for transfers between devices: 435 us -> none
    dot_general x11 -> x0, matrix products: 159 us -> none  [the longest x1 29.1 us: local_step(): jnp.einsum('tbd,fd->tbf', d_trunk, w_down, preferred_element_type=jnp.flo...]
    pallas_call x0 -> x2, Pallas kernels: none -> 138 us  [the longest x1 136 us: mega_call(): pl.pallas_call(functools.partial(mega_kernel, n_total), out_shape=[jax.Sh...]
    psum x1 -> x0, waiting for transfers between devices: 138 us -> none  [local_step(): mlp_out = lax.psum(part_out, 'model')]
    transpose x2 -> x0, local copies, waits for them, and re-layouts: 44.7 us -> none  [the longest x1 22.8 us: local_step(): jnp.einsum('bd,tbf->tdf', tokens, d_pre, preferred_element_type=jnp.float32)]
    psum x1 -> x0, blocking collectives: 30.9 us -> none  [local_step(): gram_mat = lax.psum(gram_part, ('model', 'data'))]
    reduce_sum x42 -> x0, other arithmetic: 15.3 us -> none  [the longest x20 12.4 us: eg_step(): return updated / jnp.sum(updated)]
    div x21 -> x0, other arithmetic: 13 us -> none  [the longest x20 13 us: eg_step(): return updated / jnp.sum(updated)]
  transfers between devices with their start and end apart: 2 -> 0, of which waited for: 2 -> 0; matrix products, arithmetic and copies ran while one was open for 2% -> 0% of each run, Pallas kernels for 0% -> 0%
where the time goes in v3:
time: 139 us
  Pallas kernels  138 us (99%)
    pallas_call x1, Pallas kernels, mega_call(): pl.pallas_call(functools.partial(mega_kernel, n_total), out_shape=[jax.Sh...  136 us

profile of v3, /device:TPU:1, one launch (start us, length us, event | category | flops | bytes accessed | tf_op | source)
XLA Modules:
  0.0 139.2 jit_solution(17023353671270322537)
XLA Ops:
  0.6 136.0 %shard_map.76 = (f32[8,128]{1,0:T(8,128)}, f32[96,1536]{1,0:T(8,128)}, f32[192,768]{1,0:T(8,128)}) custom-call(bf16[2048,768]{1,0:T(8,128)(2,1)} %x_hbm.1, bf16[768,1536]{1,0:T(8,128)(2,1)} %w1_hbm.1, bf16[1536,768]{1,0:T(8,128)(2,1)} %w2_hbm.1, bf16[3,4,768]{2,1,0:T(4,128)(2,1)} %bitcast.1, s32[4,2048]{1,0:T(4,128)} %lab_ref.1), custom_call_target="tpu_custom_call" | custom-call | tf_op jit(solution)/shard_map/pallas_call | solution.py:466
  136.7 2.3 %shard_map.77 = (f32[4]{0:T(128)}, f32[96,1536]{1,0:T(8,128)}, f32[192,768]{1,0:T(8,128)}) custom-call(f32[8,128]{1,0:T(8,128)} %get-tuple-element.6.wts_in, f32[96,1536]{1,0:T(8,128)} %get-tuple-element.7.g1_in, f32[192,768]{1,0:T(8,128)} %get-tuple-element.8.g2_in), custom_call_target="tpu_custom_call" | custom-call | tf_op jit(solution)/shard_map/pallas_call | solution.py:496

commit v4 on v3

--- a/solution.py
+++ b/solution.py
@@ -29,8 +29,8 @@
     a2 = a * a
     t = jnp.tanh(a * (C0 + (C0 * C1) * a2))
     h = 0.5 + 0.5 * t
-    slope = h + (0.5 * a) * (1.0 - t * t) * (C0 + (3.0 * C0 * C1) * a2)
-    return a * h, slope
+    act = a * h
+    return act, h + act * (1.0 - h) * (2.0 * C0 + (6.0 * C0 * C1) * a2)
 
 
 def nt_dot(a, b):
@@ -59,15 +59,15 @@
             dz[r0:r0 + rows, 128 * j:128 * j + 128] = val.astype(BF16)
 
 
-def act_part(x, w1t_ref, ut, sl, lo):
+def act_part(x, w1t_ref, ut, sl):
     act, slope = gelu_both(nt_dot(w1t_ref[...], x))
-    ut[:, lo:lo + x.shape[0]] = act.astype(BF16)
-    sl[:, lo:lo + x.shape[0]] = slope
+    ut[...] = act.astype(BF16)
+    sl[...] = slope
 
 
 def mega_kernel(n_total, x_hbm, w1_hbm, w2_hbm, heads_ref, lab_ref, wts_ref, out1_ref, out2_ref,
                 x_all, e_all, w1v, w2v, w1f, w2f, w1t, w2s, hb, part, act_far, g1, g2, rx1, rx2,
-                dz00, dz01, dz10, dz11, da00, da01, da10, da11, ut0, ut1, ut2, sl0, sl1, sl2, gr_own, gr_all, tr_ref, rx_g1,
+                dz00, dz01, dz10, dz11, da00, da01, da10, da11, ut_own, sl_own, gr_own, gr_all, tr_ref, rx_g1,
                 ssem, rsem, lsem, osend, orecv):
     m = lax.axis_index('model')
     d = lax.axis_index('data')
@@ -111,37 +111,39 @@
         k = table[name]
         return pltpu.make_async_remote_copy(src, dst, ssem.at[k], rsem.at[k], device_id=dev, device_id_type=MESH)
 
-    def w1_rows(dr):
-        return w1f.at[pl.ds(pl.multiple_of(xor_data(d, dr) * p1, p1), p1), :]
-
-    def w2_rows(dr):
-        return w2f.at[pl.ds(pl.multiple_of(xor_data(d, dr) * p2, p2), p2), :]
-
-    rows_of = {1: w1_rows, 2: w2_rows}
-
-    def w_copy(w, name, dr, dev):
-        return rcopy(f'w{w}{name}', rows_of[w](dr), rows_of[w](dr), dev)
-
-    wt = {1: rcopy('w1t', w1_hbm.at[pl.ds(pl.multiple_of(d * p1, p1), p1), :], w1_rows(0), twin),
-          2: rcopy('w2t', w2_hbm.at[pl.ds(pl.multiple_of(d * p2, p2), p2), :], w2_rows(0), twin)}
-    w_own = {(w, n): w_copy(w, 'own' + n, 0, dev) for w in (1, 2) for n, dev in (('p', peer), ('x', nb_x), ('y', nb_y))}
-    w_peer = {(w, dr): w_copy(w, f'peer{dr}', dr, peer) for w in (1, 2) for dr in (1, 2, 3)}
-    w_diag = {1: rcopy('w1d', w1_hbm.at[pl.ds(pl.multiple_of(xor_data(d, 3) * p1, p1), p1), :], w1_rows(3), twin),
-              2: rcopy('w2d', w2_hbm.at[pl.ds(pl.multiple_of(xor_data(d, 3) * p2, p2), p2), :], w2_rows(3), twin)}
-
-    def own_block(b, lo, n):
-        return x_hbm.at[pl.ds(pl.multiple_of(b * BLK + lo, BLK // 2), n), :]
-
-    hb2 = BLK // 2
-    first_x = [rcopy(f'fx{h}', own_block(3 * m, h * hb2, hb2), slot(4, h * hb2, hb2), nb_x) for h in (0, 1)]
-    first_y = [rcopy(f'fy{h}', own_block(1 + m, h * hb2, hb2), slot(5, h * hb2, hb2), nb_y) for h in (0, 1)]
-    more_x = [rcopy(f'mx{b}', own_block(b, 0, BLK), slot(k), nb_x) for b, k in ((1, 10), (2, 13))]
-    more_y = [rcopy(f'my{b}', own_block(b, 0, BLK), slot(k), nb_y) for b, k in ((0, 11), (3, 14))]
-    fwd_x = [rcopy(f'dx{h}', slot(5, h * hb2, hb2), slot(6, h * hb2, hb2), nb_x) for h in (0, 1)]
-    fwd_y = [rcopy(f'dy{h}', slot(4, h * hb2, hb2), slot(7, h * hb2, hb2), nb_y) for h in (0, 1)]
-    z_x = [rcopy(f'zx{h}', slot(4, h * hb2, hb2), slot(8, h * hb2, hb2), twin) for h in (0, 1)]
-    z_y = [rcopy(f'zy{h}', slot(5, h * hb2, hb2), slot(9, h * hb2, hb2), twin) for h in (0, 1)]
-    z_d = [rcopy('zd6', slot(6), slot(12), twin), rcopy('zd7', slot(7), slot(15), twin)]
+    def w_rows(w, dr, part=None, ref=None):
+        n = p1 if w == 1 else p2
+        lo, size = (0, n) if part is None else (part * (n // 2), n // 2)
+        ref = (w1f if w == 1 else w2f) if ref is None else ref
+        return ref.at[pl.ds(pl.multiple_of(xor_data(d, dr) * n + lo, n // 2), size), :]
+
+    w_hbm = {1: w1_hbm, 2: w2_hbm}
+    wt = {(w, h): rcopy(f't{w}{h}', w_rows(w, 0, h, w_hbm[w]), w_rows(w, 0, h), twin) for w in (1, 2) for h in (0, 1)}
+    wd = {1: rcopy('d1', w_rows(1, 3, 1, w1_hbm), w_rows(1, 3, 1), twin), 2: rcopy('d2', w_rows(2, 3, None, w2_hbm), w_rows(2, 3), twin)}
+    w_own = {(w, h, n): rcopy(f'o{w}{h}{n}', w_rows(w, 0, h), w_rows(w, 0, h), dev)
+             for w in (1, 2) for h in (0, 1) for n, dev in (('x', nb_x), ('y', nb_y))}
+    w_peer = {(w, dr): rcopy(f'p{w}{dr}', w_rows(w, dr), w_rows(w, dr), peer) for w in (1, 2) for dr in range(4)}
+    w_fwd = rcopy('g0', w_rows(1, 1, 0), w_rows(1, 1, 0), nb_y)
+
+    pieces = ((0, BLK // 4), (BLK // 4, BLK // 4), (BLK // 2, BLK // 2))
+
+    def own_piece(b, lo, n):
+        return x_hbm.at[pl.ds(pl.multiple_of(b * BLK + lo, BLK // 4), n), :]
+
+    def cut(name, src, dst, dev):
+        return [rcopy(f'{name}{lo}', slot(src, lo, n), slot(dst, lo, n), dev) for lo, n in pieces]
+
+    first_x = [rcopy(f'fx{lo}', own_piece(3 * m, lo, n), slot(4, lo, n), nb_x) for lo, n in pieces]
+    first_y = [rcopy(f'fy{lo}', own_piece(1 + m, lo, n), slot(5, lo, n), nb_y) for lo, n in pieces]
+    more_x = [rcopy(f'mx{b}', own_piece(b, 0, BLK), slot(k), nb_x) for b, k in ((1, 10), (2, 13))]
+    more_y = [rcopy(f'my{k}', own_piece(b, 0, BLK), slot(k), nb_y) for b, k in ((3 - 3 * m, 11), (3 * m, 14))]
+    fwd_x = cut('dx', 5, 7, nb_x)
+    fwd_y = cut('dy', 4, 8, nb_y)
+    z_x = cut('zx', 4, 6, twin)
+    z_y = cut('zy', 5, 9, twin)
+    keep15 = BLK - BLK // 4
+    z_d = [rcopy('zd7', slot(7), slot(12), twin), rcopy('zd8', slot(8, 0, keep15), slot(15, 0, keep15), twin)]
+    last_x = rcopy('lx', slot(11, keep15, BLK // 4), slot(15, keep15, BLK // 4), nb_x)
 
     k_out, k_in = m, 1 - m
     e_twin = [rcopy(f'et{k}', e_all.at[k], e_all.at[2 + k], twin) for k in range(2)]
@@ -149,27 +151,20 @@
     for dz in (0, 1):
         for dr in (1, 2, 3):
             dev = (lax.rem(m + dz, 2), xor_data(d, dr))
-            s_out, s_in = {1: (4 + 4 * dz, 10 + 3 * m), 2: (11 + 3 * m, 5 + 4 * dz), 3: (7 + 8 * dz, 6 + 6 * dz)}[dr]
+            s_out, s_in = {1: (4 + 2 * dz, 10 + 3 * m), 2: (14 - 3 * dz, 5 + 4 * dz), 3: (8 + 7 * dz, 7 + 5 * dz)}[dr]
             e_rest.append(rcopy(f'eo{dz}{dr}', e_all.at[k_out], e_all.at[s_out], dev))
             e_rest.append(rcopy(f'ei{dz}{dr}', e_all.at[k_in], e_all.at[s_in], dev))
 
-    wt[1].start()
+    wt[1, 0].start()
+    wt[1, 1].start()
     first_x[0].start()
     first_y[0].start()
-    wt[2].start()
-    w_diag[1].start()
-    w_diag[2].start()
-
-    for c in range(N_CLASS - 1):
-        h = heads_ref[c].astype(F32) - heads_ref[N_CLASS - 1].astype(F32)
-        h = jnp.concatenate([h, h], axis=0).T
-        for t in range(N_TASK):
-            hb[(N_CLASS - 1) * t + c] = jnp.broadcast_to(h[:, t:t + 1], (dim, 128))
+    wt[2, 0].start()
+    wt[2, 1].start()
+    wd[1].start()
+    wd[2].start()
     for k in range(4):
         lcopy[k].wait()
-    off = pl.multiple_of(chip * sl, sl)
-    w1t[...] = w1v[:, pl.ds(off, sl)].T
-    w2s[...] = w2v[pl.ds(off, sl), :]
 
     fc = wide // 3
 
@@ -182,63 +177,89 @@
             acc = y if acc is None else acc + y
         part[k] = acc
 
+    def act_own(k):
+        act_part(x_all[k * BLK:(k + 1) * BLK, :], w1t, ut_own.at[k], sl_own.at[k])
+
     with jax.named_scope('near'):
         part_block(0)
-        wt[1].wait_recv()
-        for n in 'xyp':
-            w_own[1, n].start()
+        wt[1, 0].wait_recv()
+        for n in 'xy':
+            w_own[1, 0, n].start()
+        for c in range(N_CLASS - 1):
+            h = heads_ref[c].astype(F32) - heads_ref[N_CLASS - 1].astype(F32)
+            h = jnp.concatenate([h, h], axis=0).T
+            for t in range(N_TASK):
+                hb[(N_CLASS - 1) * t + c] = jnp.broadcast_to(h[:, t:t + 1], (dim, 128))
+        off = pl.multiple_of(chip * sl, sl)
+        w1t[...] = w1v[:, pl.ds(off, sl)].T
+        w2s[...] = w2v[pl.ds(off, sl), :]
+        wt[1, 1].wait_recv()
+        for n in 'xy':
+            w_own[1, 1, n].start()
+        w_peer[1, 0].start()
         part_block(1)
-        wt[2].wait_recv()
-        for n in 'xyp':
-            w_own[2, n].start()
-        first_x[1].start()
-        first_y[1].start()
-        first_x[0].wait_recv()
-        z_x[0].start()
-        first_y[0].wait_recv()
-        fwd_x[0].start()
-        fwd_y[0].start()
-        act_part(x_all[0:BLK, :], w1t, ut0, sl0, 0)
-        g1[...] = jnp.zeros_like(g1)
-        g2[...] = jnp.zeros_like(g2)
+    with jax.named_scope('wait_t2'):
+        w_own[1, 0, 'x'].wait_recv()
+        w_fwd.start()
+        wt[2, 0].wait_recv()
+        for n in 'xy':
+            w_own[2, 0, n].start()
+        for n, dr, hs in (('x', 1, (1,)), ('y', 2, (0, 1))):
+            for h in hs:
+                w_own[1, h, n].wait_recv()
+            w_peer[1, dr].start()
+        wt[2, 1].wait_recv()
+        for n in 'xy':
+            w_own[2, 1, n].start()
+        w_peer[2, 0].start()
+        for j in (1, 2):
+            first_x[j].start()
+            first_y[j].start()
+    for k in (4, 5):
+        lcopy[k].wait()
+    act_own(0)
+    act_own(1)
+    first_x[0].wait_recv()
+    z_x[0].start()
+    first_y[0].wait_recv()
+    act_own(2)
+    act_own(3)
     with jax.named_scope('wait_w1'):
-        w_own[1, 'x'].wait_recv()
-        w_peer[1, 1].start()
-        w_own[1, 'y'].wait_recv()
-        w_peer[1, 2].start()
-        w_diag[1].wait_recv()
+        w_fwd.wait_recv()
+        wd[1].wait_recv()
         w_peer[1, 3].start()
-        w_own[1, 'p'].wait_recv()
-        for dr in (1, 2, 3):
+        for h in (0, 1):
+            w_own[2, h, 'x'].wait_recv()
+        w_peer[2, 1].start()
+        for dr in range(4):
             w_peer[1, dr].wait_recv()
     with jax.named_scope('far1'):
         for k in range(2):
             x = x_all[k * BLK:(k + 1) * BLK, :]
             for f in range(0, wide, fc):
                 act_far[k, :, f:f + fc] = gelu_only(nn_dot(x, w1f[:, f:f + fc])).astype(BF16)
-    def w2_chunk(k, dr):
-        rows = pl.ds(pl.multiple_of((xor_data(d, dr) // 2) * sl, sl), sl)
+    def w2_pair(k, j):
+        rows = pl.ds(pl.multiple_of(lax.rem(chip // 2 + j, 2) * (2 * sl), 2 * sl), 2 * sl)
         part[k] += nn_dot(act_far[k, :, rows], w2f[rows, :])
 
     with jax.named_scope('wait_w2'):
-        w_own[2, 'x'].wait_recv()
-        w_peer[2, 1].start()
-        w_own[2, 'y'].wait_recv()
+        for h in (0, 1):
+            w_own[2, h, 'y'].wait_recv()
         w_peer[2, 2].start()
-        w_own[2, 'p'].wait_recv()
-        for k in range(2):
-            w2_chunk(k, 0)
-        for dr in (1, 2):
+        for dr in (0, 1):
             w_peer[2, dr].wait_recv()
-            for k in range(2):
-                w2_chunk(k, dr)
-        w_diag[2].wait_recv()
+        w2_pair(0, 0)
+        wd[2].wait_recv()
         w_peer[2, 3].start()
-        w_peer[2, 3].wait_recv()
+        g1[...] = jnp.zeros_like(g1)
+        g2[...] = jnp.zeros_like(g2)
+        w2_pair(1, 0)
+        for dr in (2, 3):
+            w_peer[2, dr].wait_recv()
     with jax.named_scope('errs'):
         heads16 = jnp.concatenate([heads_ref[c] for c in range(N_CLASS)] + [heads_ref[0]], axis=0)
         for k in range(2):
-            w2_chunk(k, 3)
+            w2_pair(k, 1)
             z = (x_all[k * BLK:(k + 1) * BLK, :].astype(F32) + part[k]).astype(BF16)
             logits = nt_dot(heads16, z)
             lg = [logits[N_TASK * c:N_TASK * c + N_TASK, :] for c in range(N_CLASS)]
@@ -251,9 +272,10 @@
                 e_all[k, N_TASK * c:N_TASK * c + N_TASK, :] = jnp.where(lab == c, -rest, ex[c] / tot) * (1.0 / n_total)
         for cp in e_twin + e_rest:
             cp.start()
-        z_y[0].start()
-
-    dzs, das, uts, sls = ((dz00, dz01), (dz10, dz11)), ((da00, da01), (da10, da11)), (ut0, ut1, ut2), (sl0, sl1, sl2)
+        for cp in (z_y[0], fwd_x[0], fwd_y[0]):
+            cp.start()
+
+    dzs, das = ((dz00, dz01), (dz10, dz11)), ((da00, da01), (da10, da11))
     n_blk = x_all.shape[0] // BLK
     keep_row = pl.multiple_of(core * half, half)
     give_row = pl.multiple_of((1 - core) * half, half)
@@ -262,18 +284,30 @@
     halves = [(rcopy(f'h1{t}', g1.at[pl.ds(t * sl, sl), pl.ds(give_col, dim // 2)], rx1.at[t], peer),
                rcopy(f'h2{t}', g2.at[pl.ds(t * sl + give_row, half), :], rx2.at[t], peer)) for t in range(N_TASK)]
 
+    def relay(j):
+        for cp in (first_x[j], first_y[j]):
+            cp.wait_recv()
+        for cp in (z_x[j], z_y[j], fwd_x[j], fwd_y[j]):
+            cp.start()
+
     with jax.named_scope('lead_in'):
+        relay(1)
         dz_part(e_all, 0, 0, hb, dz00)
-        first_x[1].wait_recv()
-        first_y[1].wait_recv()
-        for cp in (fwd_x[1], fwd_y[1], z_x[1], z_y[1], more_x[0], more_y[0], more_x[1], more_y[1]):
+
+    def links_2():
+        relay(2)
+        for cp in more_x + more_y:
             cp.start()
 
-    def links_2():
-        for cp in fwd_x + fwd_y:
+    def links_6():
+        for cp in z_x + fwd_x + fwd_y:
             cp.wait_recv()
         for cp in z_d:
             cp.start()
+
+    def links_11():
+        more_y[0].wait_recv()
+        last_x.start()
 
     def arrive(*cps):
         def go():
@@ -281,10 +315,16 @@
                 cp.wait_recv()
         return go
 
-    lcopy[4].wait()
-    lcopy[5].wait()
-    actions = {1: arrive(*e_twin), 3: arrive(*e_rest), 5: links_2, 7: arrive(*z_x), 8: arrive(*z_y), 9: arrive(more_x[0]),
-               10: arrive(more_y[0]), 11: arrive(z_d[0]), 12: arrive(more_x[1]), 13: arrive(more_y[1])}
+    actions = {1: arrive(*e_twin), 2: links_2, 3: arrive(*e_rest), 6: links_6, 9: arrive(*z_y), 10: arrive(more_x[0]),
+               11: links_11, 12: arrive(z_d[0]), 13: arrive(more_x[1])}
+
+    def act_upon(s, lo, hi):
+        for k, act in actions.items():
+            if lo <= k < hi:
+                @pl.when(s == k)
+                def _():
+                    with jax.named_scope(f'arr{k}'):
+                        act()
 
     def tok(b, lo=0, n=BLK):
         return pl.ds(pl.multiple_of(b * BLK + lo, 256), n)
@@ -296,44 +336,48 @@
         return out
 
     def group(blks, nxt, last):
-        hw = BLK // 2
         for t in range(N_TASK):
             dz, da = dzs[t % 2], das[t % 2]
             rows = slice(t * sl, (t + 1) * sl)
             for b, u, h in blks:
-                da[h][...] = (nn_dot(w2s[...], dz[h][...]) * sls[u][...]).astype(BF16)
+                da[h][...] = (nn_dot(w2s[...], dz[h][...]) * sl_own[u]).astype(BF16)
             if t < N_TASK - 1:
                 for b, u, h in blks:
                     dz_part(e_all, b, t + 1, hb, dzs[(t + 1) % 2][h])
             elif nxt is not None:
-                dz_part(e_all, nxt[0], 0, hb, dzs[0][nxt[2]])
-            if t < 2 and nxt is not None:
-                act_part(x_all[tok(nxt[0], t * hw, hw), :], w1t, uts[nxt[1]], sls[nxt[1]], t * hw)
-            g2[rows, :] += total([nt_dot(uts[u][...], dz[h][...]) for b, u, h in blks])
+                dz_part(e_all, nxt, 0, hb, dzs[0][0])
+            g2[rows, :] += total([nt_dot(ut_own[u], dz[h][...]) for b, u, h in blks])
             g1[rows, :] += total([nn_dot(da[h][...], x_all[tok(b), :]) for b, u, h in blks])
-            if last:
-                for cp in halves[t]:
+            if last and t > 0:
+                for cp in (halves[t] if t > 1 else halves[0] + halves[1]):
                     cp.start()
 
-    def body(i, c):
-        for q in (0, 1):
-            for k, act in actions.items():
-                if k % 2 == q:
-                    @pl.when(i == k // 2)
-                    def _():
-                        with jax.named_scope(f'arr{k}'):
-                            act()
-            group([(2 * i + q, q, 0)], (2 * i + q + 1, 1 - q, 0), False)
+    n_own = ut_own.shape[0]
+
+    def own_body(s, c):
+        act_upon(s, 0, n_own)
+        group([(s, s, 0)], s + 1, False)
         return c
 
+    def far_body(s, c):
+        act_upon(s, n_own, n_blk)
+        act_part(x_all[tok(s), :], w1t, ut_own.at[0], sl_own.at[0])
+        group([(s, 0, 0)], s + 1, False)
+        return c
+
+    with jax.named_scope('main_own'):
+        lax.fori_loop(0, n_own, own_body, 0)
     with jax.named_scope('main'):
-        lax.fori_loop(0, n_blk // 2 - 1, body, 0)
+        lax.fori_loop(n_own, n_blk - 2, far_body, 0)
     with jax.named_scope('last_act'):
+        more_y[1].wait_recv()
         z_d[1].wait_recv()
-        act_part(x_all[tok(n_blk - 1), :], w1t, ut2, sl2, 0)
+        last_x.wait_recv()
+        act_part(x_all[tok(n_blk - 2), :], w1t, ut_own.at[0], sl_own.at[0])
+        act_part(x_all[tok(n_blk - 1), :], w1t, ut_own.at[1], sl_own.at[1])
         dz_part(e_all, n_blk - 1, 0, hb, dz01)
     with jax.named_scope('main_last'):
-        group([(n_blk - 2, 0, 0), (n_blk - 1, 2, 1)], None, True)
+        group([(n_blk - 2, 0, 0), (n_blk - 1, 1, 1)], None, True)
 
     with jax.named_scope('halves'):
         pairs = [(i, j) for i in range(N_TASK) for j in range(i, N_TASK)]
@@ -377,8 +421,8 @@
             grams.append(rcopy(f'gram{k}', gr_own, gr_all.at[me], (p // N_DATA, lax.rem(p, N_DATA))))
             grams[-1].start()
 
-        w_sends = list(wt.values()) + list(w_own.values()) + list(w_peer.values()) + list(w_diag.values())
-        for cp in (w_sends + first_x + first_y + more_x + more_y + fwd_x + fwd_y + z_x + z_y + z_d + e_twin + e_rest
+        w_sends = list(wt.values()) + list(w_own.values()) + list(w_peer.values()) + list(wd.values()) + [w_fwd]
+        for cp in (w_sends + first_x + first_y + more_x + more_y + fwd_x + fwd_y + [last_x] + z_x + z_y + z_d + e_twin + e_rest
                    + [cp for h in halves for cp in h]):
             cp.wait_send()
 
@@ -476,9 +520,9 @@
                         vmem((2, n_half // 2, dim), F32), vmem((2, n_half // 2, wide), BF16),
                         vmem((N_TASK * sl, dim), F32), vmem((N_TASK * sl, dim), F32),
                         vmem((N_TASK, sl, dim // 2), F32), vmem((N_TASK, half, dim), F32),
-                        *[vmem((dim, BLK), BF16)] * 4, *[vmem((sl, BLK), BF16)] * 7, *[vmem((sl, BLK), F32)] * 3,
+                        *[vmem((dim, BLK), BF16)] * 4, *[vmem((sl, BLK), BF16)] * 4, vmem((4, sl, BLK), BF16), vmem((4, sl, BLK), F32),
                         vmem((16, 128), F32), vmem((N_DEV, 16, 128), F32), vmem((dim // 2, sl), F32), vmem((per, wide), F32),
-                        pltpu.SemaphoreType.DMA((88,)), pltpu.SemaphoreType.DMA((88,)), pltpu.SemaphoreType.DMA((8,)),
+                        pltpu.SemaphoreType.DMA((100,)), pltpu.SemaphoreType.DMA((100,)), pltpu.SemaphoreType.DMA((8,)),
                         pltpu.SemaphoreType.DMA((4,)), pltpu.SemaphoreType.DMA((4,))],
         compiler_params=pltpu.CompilerParams(vmem_limit_bytes=VMEM_LIMIT, collective_id=0, has_side_effects=True),
     )(tokens, w_up, w_down, task_heads, labels)

time: 139 us -> 131 us (0.942)
  Pallas kernels: 138 us -> 130 us
    pallas_call x1, Pallas kernels: 136 us -> 128 us  [mega_call(): pl.pallas_call(functools.partial(mega_kernel, n_total), out_shape=[jax.Sh...]
where the time goes in v4:
time: 131 us
  Pallas kernels  130 us (99%)
    pallas_call x1, Pallas kernels, mega_call(): pl.pallas_call(functools.partial(mega_kernel, n_total), out_shape=[jax.Sh...  128 us

profile of v4, /device:TPU:1, one launch (start us, length us, event | category | flops | bytes accessed | tf_op | source)
XLA Modules:
  0.0 131.1 jit_solution(9878207366128198895)
XLA Ops:
  0.6 128.0 %shard_map.76 = (f32[8,128]{1,0:T(8,128)}, f32[96,1536]{1,0:T(8,128)}, f32[192,768]{1,0:T(8,128)}) custom-call(bf16[2048,768]{1,0:T(8,128)(2,1)} %x_hbm.1, bf16[768,1536]{1,0:T(8,128)(2,1)} %w1_hbm.1, bf16[1536,768]{1,0:T(8,128)(2,1)} %w2_hbm.1, bf16[3,4,768]{2,1,0:T(4,128)(2,1)} %bitcast.1, s32[4,2048]{1,0:T(4,128)} %lab_ref.1), custom_call_target="tpu_custom_call" | custom-call | tf_op jit(solution)/shard_map/pallas_call | solution.py:510
  128.6 2.3 %shard_map.77 = (f32[4]{0:T(128)}, f32[96,1536]{1,0:T(8,128)}, f32[192,768]{1,0:T(8,128)}) custom-call(f32[8,128]{1,0:T(8,128)} %get-tuple-element.6.wts_in, f32[96,1536]{1,0:T(8,128)} %get-tuple-element.7.g1_in, f32[192,768]{1,0:T(8,128)} %get-tuple-element.8.g2_in), custom_call_target="tpu_custom_call" | custom-call | tf_op jit(solution)/shard_map/pallas_call | solution.py:540

commit v5 on v4

--- a/solution.py
+++ b/solution.py
@@ -18,6 +18,7 @@
 N_TASK = 4
 N_CLASS = 3
 BLK = 512
+LANE = 128
 VMEM_LIMIT = 63 * 1024 * 1024
 
 
@@ -51,12 +52,12 @@
 def dz_part(e_ref, s, t, hb_ref, dz):
     dim, blk = dz.shape
     rows = 32
-    es = [[e_ref[s, N_TASK * c + t:N_TASK * c + t + 1, lo:lo + 128] for lo in range(0, blk, 128)] for c in range(N_CLASS - 1)]
+    es = [[e_ref[s, N_TASK * c + t:N_TASK * c + t + 1, lo:lo + LANE] for lo in range(0, blk, LANE)] for c in range(N_CLASS - 1)]
     for r0 in range(0, dim, rows):
         h = [hb_ref[(N_CLASS - 1) * t + c, r0:r0 + rows, :] for c in range(N_CLASS - 1)]
-        for j in range(blk // 128):
+        for j in range(blk // LANE):
             val = h[0] * es[0][j] + h[1] * es[1][j]
-            dz[r0:r0 + rows, 128 * j:128 * j + 128] = val.astype(BF16)
+            dz[r0:r0 + rows, LANE * j:LANE * j + LANE] = val.astype(BF16)
 
 
 def act_part(x, w1t_ref, ut, sl):
@@ -65,9 +66,9 @@
     sl[...] = slope
 
 
-def mega_kernel(n_total, x_hbm, w1_hbm, w2_hbm, heads_ref, lab_ref, wts_ref, out1_ref, out2_ref,
+def mega_kernel(n_total, x_hbm, w1_hbm, w2_hbm, heads_hbm, lab_hbm, wts_ref, out1_ref, out2_ref,
                 x_all, e_all, w1v, w2v, w1f, w2f, w1t, w2s, hb, part, act_far, g1, g2, rx1, rx2,
-                dz00, dz01, dz10, dz11, da00, da01, da10, da11, ut_own, sl_own, gr_own, gr_all, tr_ref, rx_g1,
+                dz00, dz01, dz10, dz11, da00, da01, da10, da11, ut_own, sl_own, gr_own, gr_all, tr_ref, rx_g1, heads_ref, lab_ref,
                 ssem, rsem, lsem, osend, orecv):
     m = lax.axis_index('model')
     d = lax.axis_index('data')
@@ -89,6 +90,7 @@
     lcopy += [pltpu.make_async_copy(w1_hbm, w1v, lsem.at[2]), pltpu.make_async_copy(w2_hbm, w2v, lsem.at[3])]
     lcopy += [pltpu.make_async_copy(x_hbm.at[pl.ds(pl.multiple_of((2 - 2 * m + k) * BLK, BLK), BLK), :], slot(2 + k),
                                     lsem.at[4 + k]) for k in range(2)]
+    lcopy += [pltpu.make_async_copy(heads_hbm, heads_ref, lsem.at[8]), pltpu.make_async_copy(lab_hbm, lab_ref, lsem.at[9])]
     for cp in lcopy:
         cp.start()
 
@@ -182,6 +184,8 @@
 
     with jax.named_scope('near'):
         part_block(0)
+        for cp in lcopy[6:]:
+            cp.wait()
         wt[1, 0].wait_recv()
         for n in 'xy':
             w_own[1, 0, n].start()
@@ -189,7 +193,7 @@
             h = heads_ref[c].astype(F32) - heads_ref[N_CLASS - 1].astype(F32)
             h = jnp.concatenate([h, h], axis=0).T
             for t in range(N_TASK):
-                hb[(N_CLASS - 1) * t + c] = jnp.broadcast_to(h[:, t:t + 1], (dim, 128))
+                hb[(N_CLASS - 1) * t + c] = jnp.broadcast_to(h[:, t:t + 1], (dim, LANE))
         off = pl.multiple_of(chip * sl, sl)
         w1t[...] = w1v[:, pl.ds(off, sl)].T
         w2s[...] = w2v[pl.ds(off, sl), :]
@@ -279,8 +283,8 @@
     n_blk = x_all.shape[0] // BLK
     keep_row = pl.multiple_of(core * half, half)
     give_row = pl.multiple_of((1 - core) * half, half)
-    keep_col = pl.multiple_of(core * (dim // 2), 128)
-    give_col = pl.multiple_of((1 - core) * (dim // 2), 128)
+    keep_col = pl.multiple_of(core * (dim // 2), LANE)
+    give_col = pl.multiple_of((1 - core) * (dim // 2), LANE)
     halves = [(rcopy(f'h1{t}', g1.at[pl.ds(t * sl, sl), pl.ds(give_col, dim // 2)], rx1.at[t], peer),
                rcopy(f'h2{t}', g2.at[pl.ds(t * sl + give_row, half), :], rx2.at[t], peer)) for t in range(N_TASK)]
 
@@ -299,8 +303,8 @@
         for cp in more_x + more_y:
             cp.start()
 
-    def links_6():
-        for cp in z_x + fwd_x + fwd_y:
+    def links_7():
+        for cp in fwd_x + fwd_y:
             cp.wait_recv()
         for cp in z_d:
             cp.start()
@@ -315,7 +319,7 @@
                 cp.wait_recv()
         return go
 
-    actions = {1: arrive(*e_twin), 2: links_2, 3: arrive(*e_rest), 6: links_6, 9: arrive(*z_y), 10: arrive(more_x[0]),
+    actions = {1: arrive(*e_twin), 2: links_2, 3: arrive(*e_rest), 6: arrive(*z_x), 7: links_7, 9: arrive(*z_y), 10: arrive(more_x[0]),
                11: links_11, 12: arrive(z_d[0]), 13: arrive(more_x[1])}
 
     def act_upon(s, lo, hi):
@@ -381,19 +385,19 @@
 
     with jax.named_scope('halves'):
         pairs = [(i, j) for i in range(N_TASK) for j in range(i, N_TASK)]
-        acc = tuple(jnp.zeros((8, 128), F32) for _ in pairs)
+        acc = tuple(jnp.zeros((8, LANE), F32) for _ in pairs)
 
         def fold(new, old, acc):
             def one(src, dst, n_rows, n_cols, row_of, col0, acc):
                 def go(r, acc):
                     row = pl.multiple_of(r * 8, 8)
                     acc = list(acc)
-                    for l in range(0, n_cols, 128):
-                        gs = {t: dst[t, pl.ds(row, 8), l:l + 128] for t in old}
+                    for l in range(0, n_cols, LANE):
+                        gs = {t: dst[t, pl.ds(row, 8), l:l + LANE] for t in old}
                         for t in new:
-                            v = dst[t, pl.ds(row, 8), l:l + 128] + src[pl.ds(pl.multiple_of(row_of(t) + row, 8), 8),
-                                                                       pl.ds(pl.multiple_of(col0 + l, 128), 128)]
-                            dst[t, pl.ds(row, 8), l:l + 128] = v
+                            v = dst[t, pl.ds(row, 8), l:l + LANE] + src[pl.ds(pl.multiple_of(row_of(t) + row, 8), 8),
+                                                                       pl.ds(pl.multiple_of(col0 + l, LANE), LANE)]
+                            dst[t, pl.ds(row, 8), l:l + LANE] = v
                             gs[t] = v
                         for q, (i, j) in enumerate(pairs):
                             if (i in new or j in new) and i in gs and j in gs:
@@ -437,7 +441,7 @@
         gram = {}
         for q, (i, j) in enumerate(pairs):
             gram[i, j] = gram[j, i] = sums[q:q + 1, :]
-        scale = (gram[0, 0] + gram[1, 1] + gram[2, 2] + gram[3, 3]) / N_TASK
+        scale = total([gram[i, i] for i in range(N_TASK)]) / N_TASK
 
         def eg_step(k, w):
             up = []
@@ -447,15 +451,15 @@
             s = (up[0] + up[1]) + (up[2] + up[3])
             return tuple(u / s for u in up)
 
-        w = lax.fori_loop(0, STEPS, eg_step, tuple(jnp.full((1, 128), 1.0 / N_TASK, F32) for _ in range(N_TASK)))
+        w = lax.fori_loop(0, STEPS, eg_step, tuple(jnp.full((1, LANE), 1.0 / N_TASK, F32) for _ in range(N_TASK)))
         wts_ref[...] = jnp.zeros_like(wts_ref)
         for t in range(N_TASK):
             wts_ref[t:t + 1, :] = w[t]
     def blend(rx, l):
-        wb = [jnp.broadcast_to(v, (rx.shape[1], 128)) for v in w]
-        v = wb[0] * rx[0, :, l:l + 128]
+        wb = [jnp.broadcast_to(v, (rx.shape[1], LANE)) for v in w]
+        v = wb[0] * rx[0, :, l:l + LANE]
         for t in range(1, N_TASK):
-            v = v + wb[t] * rx[t, :, l:l + 128]
+            v = v + wb[t] * rx[t, :, l:l + LANE]
         return v
 
     with jax.named_scope('outs'):
@@ -468,8 +472,8 @@
             outs.append((p, pltpu.make_async_remote_copy(src, rx_g1.at[:, cols], osend.at[j], orecv.at[chip],
                                                          device_id=(m, p), device_id_type=MESH),
                          pltpu.make_async_copy(src, rx_g1.at[:, cols], lsem.at[7])))
-        for l in range(0, dim // 2, 128):
-            tr_ref[l:l + 128, :] = blend(rx1, l).T
+        for l in range(0, dim // 2, LANE):
+            tr_ref[l:l + LANE, :] = blend(rx1, l).T
         for p, far, near in outs:
             @pl.when(p != d)
             def _():
@@ -478,8 +482,8 @@
             @pl.when(p == d)
             def _():
                 near.start()
-        for l in range(0, dim, 128):
-            out2_ref[:, l:l + 128] = blend(rx2, l)
+        for l in range(0, dim, LANE):
+            out2_ref[:, l:l + LANE] = blend(rx2, l)
         for k in range(N_DATA // 2):
             @pl.when(jnp.logical_or(core != d // n_dest, chip != k))
             def _():
@@ -509,20 +513,21 @@
     vmem = pltpu.VMEM
     return pl.pallas_call(
         functools.partial(mega_kernel, n_total),
-        out_shape=[jax.ShapeDtypeStruct((8, 128), F32), jax.ShapeDtypeStruct((per, half * N_DATA), F32),
+        out_shape=[jax.ShapeDtypeStruct((8, LANE), F32), jax.ShapeDtypeStruct((per, half * N_DATA), F32),
                    jax.ShapeDtypeStruct((half, dim), F32)],
-        in_specs=[hbm, hbm, hbm, vm, vm],
+        in_specs=[hbm] * 5,
         out_specs=[vm, vm, vm],
         scratch_shapes=[vmem((4 * n_loc, dim), BF16), vmem((4 * n_loc // BLK, 8, BLK), F32),
                         vmem((dim, wide), BF16), vmem((wide, dim), BF16), vmem((dim, wide), BF16), vmem((wide, dim), BF16),
                         vmem((sl, dim), BF16), vmem((sl, dim), BF16),
-                        vmem((N_TASK * (N_CLASS - 1), dim, 128), F32),
+                        vmem((N_TASK * (N_CLASS - 1), dim, LANE), F32),
                         vmem((2, n_half // 2, dim), F32), vmem((2, n_half // 2, wide), BF16),
                         vmem((N_TASK * sl, dim), F32), vmem((N_TASK * sl, dim), F32),
                         vmem((N_TASK, sl, dim // 2), F32), vmem((N_TASK, half, dim), F32),
                         *[vmem((dim, BLK), BF16)] * 4, *[vmem((sl, BLK), BF16)] * 4, vmem((4, sl, BLK), BF16), vmem((4, sl, BLK), F32),
-                        vmem((16, 128), F32), vmem((N_DEV, 16, 128), F32), vmem((dim // 2, sl), F32), vmem((per, wide), F32),
-                        pltpu.SemaphoreType.DMA((100,)), pltpu.SemaphoreType.DMA((100,)), pltpu.SemaphoreType.DMA((8,)),
+                        vmem((16, LANE), F32), vmem((N_DEV, 16, LANE), F32), vmem((dim // 2, sl), F32), vmem((per, wide), F32),
+                        vmem(task_heads.shape, BF16), vmem(labels.shape, jnp.int32),
+                        pltpu.SemaphoreType.DMA((100,)), pltpu.SemaphoreType.DMA((100,)), pltpu.SemaphoreType.DMA((10,)),
                         pltpu.SemaphoreType.DMA((4,)), pltpu.SemaphoreType.DMA((4,))],
         compiler_params=pltpu.CompilerParams(vmem_limit_bytes=VMEM_LIMIT, collective_id=0, has_side_effects=True),
     )(tokens, w_up, w_down, task_heads, labels)

time: 131 us -> 131 us (level)
  no operation moved by 1% of the time
where the time goes in v5:
time: 131 us; the launch traced here: 130 us
  Pallas kernels  130 us (99%)
    pallas_call x1, Pallas kernels, mega_call(): pl.pallas_call(functools.partial(mega_kernel, n_total), out_shape=[jax.Sh...  127 us

profile of v5, /device:TPU:1, one launch (start us, length us, event | category | flops | bytes accessed | tf_op | source)
XLA Modules:
  0.0 130.5 jit_solution(18418976714475115122)
XLA Ops:
  0.6 127.4 %shard_map.76 = (f32[8,128]{1,0:T(8,128)}, f32[96,1536]{1,0:T(8,128)}, f32[192,768]{1,0:T(8,128)}) custom-call(bf16[2048,768]{1,0:T(8,128)(2,1)} %x_hbm.1, bf16[768,1536]{1,0:T(8,128)(2,1)} %w1_hbm.1, bf16[1536,768]{1,0:T(8,128)(2,1)} %w2_hbm.1, bf16[3,4,768]{2,1,0:T(4,128)(2,1)} %bitcast.1, s32[4,2048]{1,0:T(4,128)} %lab_hbm.1), custom_call_target="tpu_custom_call" | custom-call | tf_op jit(solution)/shard_map/pallas_call | solution.py:514
  128.0 2.3 %shard_map.77 = (f32[4]{0:T(128)}, f32[96,1536]{1,0:T(8,128)}, f32[192,768]{1,0:T(8,128)}) custom-call(f32[8,128]{1,0:T(8,128)} %get-tuple-element.6.wts_in, f32[96,1536]{1,0:T(8,128)} %get-tuple-element.7.g1_in, f32[192,768]{1,0:T(8,128)} %get-tuple-element.8.g2_in), custom_call_target="tpu_custom_call" | custom-call | tf_op jit(solution)/shard_map/pallas_call | solution.py:545

commit v6 on v5

--- a/solution.py
+++ b/solution.py
@@ -127,10 +127,11 @@
     w_peer = {(w, dr): rcopy(f'p{w}{dr}', w_rows(w, dr), w_rows(w, dr), peer) for w in (1, 2) for dr in range(4)}
     w_fwd = rcopy('g0', w_rows(1, 1, 0), w_rows(1, 1, 0), nb_y)
 
-    pieces = ((0, BLK // 4), (BLK // 4, BLK // 4), (BLK // 2, BLK // 2))
+    lead = 5 * BLK // 16
+    pieces = ((0, lead), (lead, BLK // 2 - lead), (BLK // 2, BLK // 2))
 
     def own_piece(b, lo, n):
-        return x_hbm.at[pl.ds(pl.multiple_of(b * BLK + lo, BLK // 4), n), :]
+        return x_hbm.at[pl.ds(pl.multiple_of(b * BLK + lo, BLK // 16), n), :]
 
     def cut(name, src, dst, dev):
         return [rcopy(f'{name}{lo}', slot(src, lo, n), slot(dst, lo, n), dev) for lo, n in pieces]
@@ -143,9 +144,9 @@
     fwd_y = cut('dy', 4, 8, nb_y)
     z_x = cut('zx', 4, 6, twin)
     z_y = cut('zy', 5, 9, twin)
-    keep15 = BLK - BLK // 4
+    keep15 = BLK - lead
     z_d = [rcopy('zd7', slot(7), slot(12), twin), rcopy('zd8', slot(8, 0, keep15), slot(15, 0, keep15), twin)]
-    last_x = rcopy('lx', slot(11, keep15, BLK // 4), slot(15, keep15, BLK // 4), nb_x)
+    last_x = rcopy('lx', slot(11, keep15, lead), slot(15, keep15, lead), nb_x)
 
     k_out, k_in = m, 1 - m
     e_twin = [rcopy(f'et{k}', e_all.at[k], e_all.at[2 + k], twin) for k in range(2)]
@@ -291,7 +292,7 @@
     def relay(j):
         for cp in (first_x[j], first_y[j]):
             cp.wait_recv()
-        for cp in (z_x[j], z_y[j], fwd_x[j], fwd_y[j]):
+        for cp in (z_x[j], fwd_x[j], fwd_y[j]):
             cp.start()
 
     with jax.named_scope('lead_in'):
@@ -300,7 +301,7 @@
 
     def links_2():
         relay(2)
-        for cp in more_x + more_y:
+        for cp in z_y[1:] + more_x + more_y:
             cp.start()
 
     def links_7():
@@ -351,9 +352,11 @@
             elif nxt is not None:
                 dz_part(e_all, nxt, 0, hb, dzs[0][0])
             g2[rows, :] += total([nt_dot(ut_own[u], dz[h][...]) for b, u, h in blks])
+            if last and t == N_TASK - 1:
+                halves[t][1].start()
             g1[rows, :] += total([nn_dot(da[h][...], x_all[tok(b), :]) for b, u, h in blks])
             if last and t > 0:
-                for cp in (halves[t] if t > 1 else halves[0] + halves[1]):
+                for cp in (halves[0] + halves[1], halves[2], halves[3][:1])[t - 1]:
                     cp.start()
 
     n_own = ut_own.shape[0]
@@ -375,9 +378,9 @@
         lax.fori_loop(n_own, n_blk - 2, far_body, 0)
     with jax.named_scope('last_act'):
         more_y[1].wait_recv()
+        act_part(x_all[tok(n_blk - 2), :], w1t, ut_own.at[0], sl_own.at[0])
         z_d[1].wait_recv()
         last_x.wait_recv()
-        act_part(x_all[tok(n_blk - 2), :], w1t, ut_own.at[0], sl_own.at[0])
         act_part(x_all[tok(n_blk - 1), :], w1t, ut_own.at[1], sl_own.at[1])
         dz_part(e_all, n_blk - 1, 0, hb, dz01)
     with jax.named_scope('main_last'):

time: 131 us -> 129 us (0.985)
  Pallas kernels: 130 us -> 128 us
    pallas_call x1, Pallas kernels: 127 us -> 126 us  [mega_call(): pl.pallas_call(functools.partial(mega_kernel, n_total), out_shape=[jax.Sh...]
where the time goes in v6:
time: 129 us
  Pallas kernels  128 us (99%)
    pallas_call x1, Pallas kernels, mega_call(): pl.pallas_call(functools.partial(mega_kernel, n_total), out_shape=[jax.Sh...  126 us

profile of v6, /device:TPU:1, one launch (start us, length us, event | category | flops | bytes accessed | tf_op | source)
XLA Modules:
  0.0 129.1 jit_solution(4388133876268207926)
XLA Ops:
  0.6 126.0 %shard_map.76 = (f32[8,128]{1,0:T(8,128)}, f32[96,1536]{1,0:T(8,128)}, f32[192,768]{1,0:T(8,128)}) custom-call(bf16[2048,768]{1,0:T(8,128)(2,1)} %x_hbm.1, bf16[768,1536]{1,0:T(8,128)(2,1)} %w1_hbm.1, bf16[1536,768]{1,0:T(8,128)(2,1)} %w2_hbm.1, bf16[3,4,768]{2,1,0:T(4,128)(2,1)} %bitcast.1, s32[4,2048]{1,0:T(4,128)} %lab_hbm.1), custom_call_target="tpu_custom_call" | custom-call | tf_op jit(solution)/shard_map/pallas_call | solution.py:517
  126.6 2.3 %shard_map.77 = (f32[4]{0:T(128)}, f32[96,1536]{1,0:T(8,128)}, f32[192,768]{1,0:T(8,128)}) custom-call(f32[8,128]{1,0:T(8,128)} %get-tuple-element.6.wts_in, f32[96,1536]{1,0:T(8,128)} %get-tuple-element.7.g1_in, f32[192,768]{1,0:T(8,128)} %get-tuple-element.8.g2_in), custom_call_target="tpu_custom_call" | custom-call | tf_op jit(solution)/shard_map/pallas_call | solution.py:548
